TPU v7x, 32 devices: a whole 2x2x4 slice. The times are simulated.
32 devices in a mesh: sec: 2 (over x), tile: 16 (over z, y, core).
Axes of the slice: x: 2, y: 2, z: 4, core: 2. Of those that a mesh axis runs over, the one named last changes fastest.
Arguments:
- atmosphere: bfloat16 [32, 360, 384], P(('sec', 'tile')), may hold values from -6 to 6
- ocean_state: bfloat16 [128, 1440, 128], P('tile', 'sec'), may hold values from -6 to 6
- land_mask: int32 [128, 1440], P('tile', 'sec'), may hold values 0 or 1
- crossing_bands: int32 [16, 4], P('tile'), may hold values from 0 to 31, as said below
- ocean_regrid: float32 [16, 4, 8, 1], P('tile'), may hold values from 0 to 1, as said below
- atmosphere_regrid: float32 [16, 4, 1, 8], P('tile'), may hold values from 0 to 1, as said below
- surface_read: bfloat16 [128], replicated, may hold values from -0.5 to 0.5
- surface_embed: float32 [384], replicated, may hold values from -4 to 4
- flux_read: bfloat16 [384, 8], replicated, may hold values from -0.3125 to 0.3125
- flux_embed: bfloat16 [8, 128], replicated, may hold values from -2 to 2
- legendre_forward: bfloat16 [128, 32, 32], P(('sec', 'tile')), may hold values from -1 to 1
- legendre_inverse: bfloat16 [128, 32, 32], P(('sec', 'tile')), may hold values from -1 to 1
- spectral_mix: bfloat16 [2, 384, 384], replicated, may hold values from -0.3125 to 0.3125
- conv_kernel: bfloat16 [2, 7, 7, 128], replicated, may hold values from -0.875 to 0.875
- norm_gain: float32 [2, 128], replicated, may hold values from 0.1 to 1.9
- expand_weight: bfloat16 [2, 128, 512], replicated, may hold values from -0.5 to 0.5
- project_weight: bfloat16 [2, 512, 128], replicated, may hold values from -0.25 to 0.25
- atmosphere_cotangent: bfloat16 [32, 360, 384], P(('sec', 'tile')), may hold values from -6 to 6
- ocean_cotangent: bfloat16 [128, 1440, 128], P('tile', 'sec'), may hold values from -6 to 6
Outputs:
- atmosphere_next: bfloat16 [32, 360, 384], P(('sec', 'tile'))
- ocean_next: bfloat16 [128, 1440, 128], P('tile', 'sec')
- atmosphere_grad: float32 [32, 360, 384], P(('sec', 'tile'))
- ocean_grad: float32 [128, 1440, 128], P('tile', 'sec')
Inputs may be any that keep to these rules, and one draw needn't show every extreme that they name: `crossing_bands`: row j lists between 1 and 4 consecutive distinct atmosphere bands, then repeats its last band; some row lists 4. Its first band is j * 2 - 1, j * 2 or j * 2 + 1, raised to 0 or lowered as far as needed for the list to end at band 32 - 1 at most. `ocean_regrid`: zero in the repeated slots of crossing_bands; the entries of each ocean row sum to one. `atmosphere_regrid`: zero in the repeated slots of crossing_bands.
All inputs are finite; a program needn't handle non-finite values. No bound on the sum of `land_mask` on one device may be relied on, other than what follows from the above.
Results may differ from a plain program's by a relative error of at most 0.008.
Values may be sent and summed in bfloat16 or wider, within the bound.
A program may use at most 128 MiB of HBM per device.

v0:
```python
import jax
import jax.numpy as jnp
from jax import lax
from jax.experimental import pallas as pl
from jax.experimental.pallas import tpu as pltpu
from jax.sharding import PartitionSpec as P


def with_halo(x, sides, width, wrap):
    for axis, dim in sides:
        size, length = (lax.axis_size(axis), x.shape[dim])
        up = [(i, (i + 1) % size) for i in range(size if wrap else size - 1)]
        down = [(j, i) for i, j in up]
        last = lax.slice_in_dim(x, length - width, length, axis=dim)
        first = lax.slice_in_dim(x, 0, width, axis=dim)
        before = lax.ppermute(last, axis, up)
        after = lax.ppermute(first, axis, down)
        x = jnp.concatenate([before, x, after], axis=dim)
    return x


def wave_table(lon_count, mode_count):
    longitude = jnp.arange(lon_count, dtype=jnp.int32)
    wavenumber = jnp.arange(mode_count, dtype=jnp.int32)
    phase = (longitude[:, None] * wavenumber[None, :] % lon_count).astype(jnp.float32) * (
        2.0 * jnp.pi / lon_count
    )
    scaled = jnp.stack([jnp.cos(phase), -jnp.sin(phase)], axis=2) * jnp.sqrt(
        jnp.float32(2.0 / lon_count)
    )
    return scaled.reshape(lon_count, 2 * mode_count).astype(jnp.bfloat16)


GELU_SCALE = 0.7978845608028654
GELU_CUBIC = 0.044715


def conv_into(window, taps, store, side):
    rows = window.shape[0] - side + 1
    extent = window.shape[1] - side + 1

    def step(index, carry):
        start = pl.multiple_of(index * 8, 8)
        totals = [None] * rows
        for col in range(side):
            weights = [taps[row * side + col] for row in range(side)]
            for line in range(rows + side - 1):
                piece = window[line, pl.ds(start + col, 8), :]
                for row in range(side):
                    target = line - row
                    if 0 <= target < rows:
                        term = piece * weights[row]
                        totals[target] = term if totals[target] is None else totals[target] + term
        for row in range(rows):
            store(row, start, totals[row])
        return carry

    lax.fori_loop(0, extent // 8, step, jnp.int32(0))


def widen(narrow, wide):
    def step(line, carry):
        wide[line] = narrow[line].astype(jnp.float32)
        return carry

    lax.fori_loop(0, narrow.shape[0], step, jnp.int32(0))


def forward_kernel(
    narrow, taps, mask, gain, expand, project, state_out, hidden_out, window
):
    widen(narrow, window)
    rows, extent, _ = state_out.shape
    side = window.shape[0] - rows + 1
    radius = side // 2

    def store(row, start, value):
        hidden_out[row, pl.ds(start, 8), :] = value

    conv_into(window, taps, store, side)

    def cells(row, carry):
        hidden = hidden_out[row]
        center = hidden - jnp.mean(hidden, axis=-1, keepdims=True)
        inverse_std = lax.rsqrt(jnp.mean(center * center, axis=-1, keepdims=True) + 1e-06)
        normed = (center * inverse_std * gain[...]).astype(jnp.bfloat16)
        before = jnp.dot(normed, expand[...], preferred_element_type=jnp.float32)
        inner = before * (GELU_SCALE + (GELU_SCALE * GELU_CUBIC) * (before * before))
        scaled = 0.5 * before
        active = (scaled + scaled * jnp.tanh(inner)).astype(jnp.bfloat16)
        update = jnp.dot(active, project[...], preferred_element_type=jnp.float32)
        old = window[row + radius, radius : radius + extent, :]
        state_out[row] = (old + mask[row].astype(jnp.float32) * update).astype(jnp.bfloat16)
        return carry

    lax.fori_loop(0, rows, cells, jnp.int32(0))


def cell_backward(hidden, cotangent, mask, gain, expand, expand_t, project_t):
    center = hidden - jnp.mean(hidden, axis=-1, keepdims=True)
    inverse_std = lax.rsqrt(jnp.mean(center * center, axis=-1, keepdims=True) + 1e-06)
    unit = center * inverse_std
    normed = (unit * gain).astype(jnp.bfloat16)
    before = jnp.dot(normed, expand, preferred_element_type=jnp.float32)
    masked = (mask.astype(jnp.float32) * cotangent).astype(jnp.bfloat16)
    active_adjoint = jnp.dot(masked, project_t, preferred_element_type=jnp.float32)
    square = before * before
    wave = jnp.tanh(before * (GELU_SCALE + (GELU_SCALE * GELU_CUBIC) * square))
    slope = (0.5 * GELU_SCALE + (1.5 * GELU_SCALE * GELU_CUBIC) * square) * before
    derivative = 0.5 + 0.5 * wave + slope * (1.0 - wave * wave)
    before_adjoint = (derivative * active_adjoint).astype(jnp.bfloat16)
    scaled = jnp.dot(before_adjoint, expand_t, preferred_element_type=jnp.float32) * gain
    return (
        inverse_std
        * (
            scaled
            - jnp.mean(scaled, axis=-1, keepdims=True)
            - unit * jnp.mean(scaled * unit, axis=-1, keepdims=True)
        )
    ).astype(jnp.bfloat16)


def backward_kernel(hidden, cotangent, mask, gain, expand, expand_t, project_t, adjoint_out):
    def cells(row, carry):
        adjoint_out[row] = cell_backward(
            hidden[row],
            cotangent[row].astype(jnp.float32),
            mask[row],
            gain[...],
            expand[...],
            expand_t[...],
            project_t[...],
        )
        return carry

    lax.fori_loop(0, hidden.shape[0], cells, jnp.int32(0))


def adjoint_kernel(narrow, taps, cotangent, cotangent_out, window):
    widen(narrow, window)
    side = window.shape[0] - cotangent.shape[0] + 1

    def store(row, start, value):
        old = cotangent[row, pl.ds(start, 8), :].astype(jnp.float32)
        cotangent_out[row, pl.ds(start, 8), :] = old + value

    conv_into(window, taps, store, side)


def adjoint_backward_kernel(
    narrow, taps, cotangent, hidden, mask, gain, expand, expand_t, project_t,
    cotangent_out, adjoint_out, window,
):
    adjoint_kernel(narrow, taps, cotangent, cotangent_out, window)
    backward_kernel(
        hidden, cotangent_out, mask, gain, expand, expand_t, project_t, adjoint_out
    )


def run_kernel(kernel, outs, flops, *operands, scratch=()):
    size = sum(x.size * x.dtype.itemsize for x in operands)
    return pl.pallas_call(
        kernel,
        out_shape=outs,
        in_specs=[pl.BlockSpec(memory_space=pltpu.VMEM)] * len(operands),
        scratch_shapes=list(scratch),
        out_specs=jax.tree.map(lambda _: pl.BlockSpec(memory_space=pltpu.VMEM), outs),
        cost_estimate=pl.CostEstimate(flops=flops, bytes_accessed=size, transcendentals=0),
    )(*operands)


def tap_tiles(kernel):
    side, _, channels = kernel.shape
    flat = kernel.astype(jnp.float32).reshape(side * side, 1, channels)
    return jnp.broadcast_to(flat, (side * side, 8, channels))


def ocean_matrix(bands_row, blocks, lat_count):
    lat_band = blocks.shape[2]
    index = bands_row[:, None] * lat_band + jnp.arange(lat_band, dtype=jnp.int32)[None, :]
    onehot = (index[:, :, None] == jnp.arange(lat_count, dtype=jnp.int32)[None, None, :]).astype(
        jnp.float32
    )
    return jnp.einsum("poi,pia->oa", blocks, onehot, precision=lax.Precision.HIGHEST)


def atmosphere_matrix(bands_row, blocks, lat_count):
    lat_band = blocks.shape[1]
    index = bands_row[:, None] * lat_band + jnp.arange(lat_band, dtype=jnp.int32)[None, :]
    onehot = (index[:, :, None] == jnp.arange(lat_count, dtype=jnp.int32)[None, None, :]).astype(
        jnp.float32
    )
    return jnp.einsum("pio,pia->ao", blocks, onehot, precision=lax.Precision.HIGHEST)


def mix_complex(coefficient, mix_real, mix_imag):
    real_part = coefficient[:, :, 0]
    imag_part = coefficient[:, :, 1]
    out_real = jnp.einsum(
        "lmc,cd->lmd", real_part, mix_real, preferred_element_type=jnp.float32
    ) - jnp.einsum("lmc,cd->lmd", imag_part, mix_imag, preferred_element_type=jnp.float32)
    out_imag = jnp.einsum(
        "lmc,cd->lmd", imag_part, mix_real, preferred_element_type=jnp.float32
    ) + jnp.einsum("lmc,cd->lmd", real_part, mix_imag, preferred_element_type=jnp.float32)
    return jnp.stack([out_real, out_imag], axis=2).astype(jnp.bfloat16)


def spectral_block(spectrum, forward, inverse, mixing):
    lat_count, columns, channels = spectrum.shape
    split = spectrum.reshape(lat_count, columns // 2, 2, channels)
    coefficient = jnp.einsum(
        "mla,amrc->lmrc", forward, split, preferred_element_type=jnp.float32
    ).astype(jnp.bfloat16)
    mixed = mix_complex(coefficient, mixing[0], mixing[1])
    returned = jnp.einsum(
        "mal,lmrc->amrc", inverse, mixed, preferred_element_type=jnp.float32
    ).astype(jnp.bfloat16)
    return returned.reshape(lat_count, columns, channels)


def spectral_adjoint(returned_adjoint, forward, inverse, mixing):
    lat_count, columns, channels = returned_adjoint.shape
    split = returned_adjoint.reshape(lat_count, columns // 2, 2, channels)
    mixed_adjoint = jnp.einsum(
        "mal,amrc->lmrc", inverse, split, preferred_element_type=jnp.float32
    ).astype(jnp.bfloat16)
    real_part = mixed_adjoint[:, :, 0]
    imag_part = mixed_adjoint[:, :, 1]
    back_real = jnp.einsum(
        "lmd,cd->lmc", real_part, mixing[0], preferred_element_type=jnp.float32
    ) + jnp.einsum("lmd,cd->lmc", imag_part, mixing[1], preferred_element_type=jnp.float32)
    back_imag = jnp.einsum(
        "lmd,cd->lmc", imag_part, mixing[0], preferred_element_type=jnp.float32
    ) - jnp.einsum("lmd,cd->lmc", real_part, mixing[1], preferred_element_type=jnp.float32)
    coefficient_adjoint = jnp.stack([back_real, back_imag], axis=2).astype(jnp.bfloat16)
    spectrum_adjoint = jnp.einsum(
        "mla,lmrc->amrc", forward, coefficient_adjoint, preferred_element_type=jnp.float32
    ).astype(jnp.bfloat16)
    return spectrum_adjoint.reshape(lat_count, columns, channels)


def to_modes(values):
    return lax.all_to_all(values, ("sec", "tile"), split_axis=1, concat_axis=0, tiled=True)


def to_bands(values):
    return lax.all_to_all(values, ("sec", "tile"), split_axis=0, concat_axis=1, tiled=True)


def rims(values, width):
    with_rows = with_halo(values, (("tile", 0),), width, False)
    return with_halo(with_rows, (("sec", 1),), width, True)


def swap(values):
    return lax.all_to_all(values, ("sec", "tile"), split_axis=0, concat_axis=0, tiled=True)


def for_halves(values, sections):
    lat_rows = values.shape[0]
    parts = jnp.moveaxis(values.reshape(lat_rows, sections, -1), 1, 0)
    tiles = lax.axis_size("tile")
    spread = jnp.broadcast_to(parts[:, None], (sections, tiles) + parts.shape[1:])
    return spread.reshape((sections * tiles,) + parts.shape[1:])


def sum_halves(received, sections):
    count, lat_rows, width = received.shape
    total = received.reshape(sections, count // sections, lat_rows, width).sum(axis=1)
    return jnp.moveaxis(total, 0, 1).reshape(lat_rows, sections * width)


def per_device(
    atmosphere,
    ocean_state,
    land_mask,
    crossing_bands,
    ocean_regrid,
    atmosphere_regrid,
    surface_read,
    surface_embed,
    flux_read,
    flux_embed,
    legendre_forward,
    legendre_inverse,
    spectral_mix,
    conv_kernel,
    norm_gain,
    expand_weight,
    project_weight,
    atmosphere_cotangent,
    ocean_cotangent,
):
    band_total = lax.axis_size(("sec", "tile"))
    lat_rows, lon_count, channels = atmosphere.shape
    lat_count = lat_rows * band_total
    ocean_rows, ocean_lon, ocean_channels = ocean_state.shape
    half = lon_count // lax.axis_size("sec")
    ratio = ocean_lon // half
    flux_count = flux_read.shape[1]
    radius = conv_kernel.shape[1] // 2
    layer_count = conv_kernel.shape[0]
    highest = lax.Precision.HIGHEST
    mask_value = land_mask.astype(jnp.float32)
    to_ocean = ocean_matrix(crossing_bands[0], ocean_regrid[0], lat_count)
    to_atmosphere = atmosphere_matrix(crossing_bands[0], atmosphere_regrid[0], lat_count)
    surface = jnp.dot(ocean_state, surface_read, preferred_element_type=jnp.float32)
    coarse = jnp.mean((mask_value * surface).reshape(ocean_rows, half, ratio), axis=2)
    sections = lax.axis_size("sec")
    flux = jnp.einsum("agc,cf->agf", atmosphere, flux_read, preferred_element_type=jnp.float32)
    coarse_parts = jnp.dot(to_atmosphere, coarse, precision=highest)
    arrived = swap(
        jnp.concatenate(
            [
                for_halves(flux.reshape(lat_rows, lon_count * flux_count), sections),
                coarse_parts.reshape(band_total, lat_rows, half),
            ],
            axis=2,
        )
    )
    flux_width = half * flux_count
    surface_atmosphere = sum_halves(arrived[:, :, flux_width:], sections)
    flux_ocean = jnp.dot(
        to_ocean, arrived[:, :, :flux_width].reshape(lat_count, flux_width), precision=highest
    )
    mixed_input = (
        atmosphere.astype(jnp.float32)
        + surface_atmosphere[:, :, None] * surface_embed[None, None, :]
    ).astype(jnp.bfloat16)
    table = wave_table(lon_count, legendre_forward.shape[0] * band_total)
    spectrum = jnp.einsum(
        "gk,agc->akc", table, mixed_input, preferred_element_type=jnp.float32
    ).astype(jnp.bfloat16)
    returned = to_bands(
        spectral_block(to_modes(spectrum), legendre_forward, legendre_inverse, spectral_mix)
    )
    response = jnp.einsum("gk,akc->agc", table, returned, preferred_element_type=jnp.float32)
    atmosphere_next = (mixed_input.astype(jnp.float32) + jax.nn.gelu(response)).astype(jnp.bfloat16)
    forcing_coarse = jnp.einsum(
        "ogf,fc->ogc",
        flux_ocean.reshape(ocean_rows, half, flux_count),
        flux_embed.astype(jnp.float32),
        precision=highest,
    )
    forcing = jnp.broadcast_to(
        forcing_coarse[:, :, None, :], (ocean_rows, half, ratio, ocean_channels)
    ).reshape(ocean_rows, ocean_lon, ocean_channels)
    state = (ocean_state.astype(jnp.float32) + mask_value[:, :, None] * forcing).astype(
        jnp.bfloat16
    )
    mask_wide = jnp.broadcast_to(
        mask_value[:, :, None], (ocean_rows, ocean_lon, ocean_channels)
    ).astype(jnp.bfloat16)
    shape = (ocean_rows, ocean_lon, ocean_channels)
    narrow = jax.ShapeDtypeStruct(shape, jnp.bfloat16)
    wide = jax.ShapeDtypeStruct(shape, jnp.float32)
    hidden_units = expand_weight.shape[2]
    work = ocean_rows * ocean_lon * ocean_channels
    conv_flops = 2000 * work
    cell_flops = 8 * work * hidden_units
    gains = norm_gain[:, None, :]
    hiddens = []
    window_scratch = (
        pltpu.VMEM(
            (ocean_rows + 2 * radius, ocean_lon + 2 * radius, ocean_channels), jnp.float32
        ),
    )
    for layer in range(layer_count):
        state, hidden = run_kernel(
            forward_kernel,
            (narrow, wide),
            conv_flops + cell_flops,
            rims(state, radius),
            tap_tiles(conv_kernel[layer]),
            mask_wide,
            gains[layer],
            expand_weight[layer],
            project_weight[layer],
            scratch=window_scratch,
        )
        hiddens.append(hidden)

    def cell_operands(layer):
        return (
            mask_wide,
            gains[layer],
            expand_weight[layer],
            expand_weight[layer].T,
            project_weight[layer].T,
        )

    def conv_operands(layer, adjoint):
        return (
            rims(adjoint, radius),
            tap_tiles(conv_kernel[layer, ::-1, ::-1]),
        )

    last = layer_count - 1
    cotangent = ocean_cotangent
    hidden_adjoint = run_kernel(
        backward_kernel,
        narrow,
        2 * cell_flops,
        hiddens[last],
        cotangent,
        *cell_operands(last),
    )
    for layer in range(last, 0, -1):
        cotangent, hidden_adjoint = run_kernel(
            adjoint_backward_kernel,
            (wide, narrow),
            conv_flops + 2 * cell_flops,
            *conv_operands(layer, hidden_adjoint),
            cotangent,
            hiddens[layer - 1],
            *cell_operands(layer - 1),
            scratch=window_scratch,
        )
    cotangent = run_kernel(
        adjoint_kernel,
        wide,
        conv_flops,
        *conv_operands(0, hidden_adjoint),
        cotangent,
        scratch=window_scratch,
    )
    forcing_adjoint = (
        (mask_value[:, :, None] * cotangent)
        .reshape(ocean_rows, half, ratio, ocean_channels)
        .sum(axis=2)
    )
    flux_ocean_adjoint = jnp.einsum(
        "ogc,fc->ogf", forcing_adjoint, flux_embed.astype(jnp.float32), precision=highest
    )
    flux_parts = jnp.dot(
        to_ocean.T, flux_ocean_adjoint.reshape(ocean_rows, flux_width), precision=highest
    )
    flux_adjoint = sum_halves(
        swap(flux_parts.reshape(band_total, lat_rows, flux_width)), sections
    ).reshape(lat_rows, lon_count, flux_count)
    from_flux = jnp.einsum(
        "agf,cf->agc", flux_adjoint, flux_read.astype(jnp.float32), precision=highest
    )
    atmosphere_adjoint = atmosphere_cotangent.astype(jnp.float32)
    _, gelu_back = jax.vjp(jax.nn.gelu, response)
    response_adjoint = gelu_back(atmosphere_adjoint)[0].astype(jnp.bfloat16)
    returned_adjoint = jnp.einsum(
        "gk,agc->akc", table, response_adjoint, preferred_element_type=jnp.float32
    ).astype(jnp.bfloat16)
    spectrum_adjoint = to_bands(
        spectral_adjoint(
            to_modes(returned_adjoint), legendre_forward, legendre_inverse, spectral_mix
        )
    )
    input_adjoint = atmosphere_adjoint + jnp.einsum(
        "gk,akc->agc", table, spectrum_adjoint, preferred_element_type=jnp.float32
    )
    atmosphere_grad = input_adjoint + from_flux
    surface_adjoint = jnp.einsum("agc,c->ag", input_adjoint, surface_embed, precision=highest)
    coarse_adjoint = jnp.dot(
        to_atmosphere.T,
        swap(for_halves(surface_adjoint, sections)).reshape(lat_count, half),
        precision=highest,
    )
    widened_adjoint = jnp.broadcast_to(
        coarse_adjoint[:, :, None], (ocean_rows, half, ratio)
    ).reshape(ocean_rows, ocean_lon)
    surface_grad = mask_value * widened_adjoint / ratio
    ocean_grad = (
        cotangent + surface_grad[:, :, None] * surface_read.astype(jnp.float32)[None, None, :]
    )
    return (atmosphere_next, state, atmosphere_grad, ocean_grad)


def solution(mesh):
    return jax.shard_map(
        per_device,
        mesh=mesh,
        in_specs=(
            P(("sec", "tile"), None, None),
            P("tile", "sec", None),
            P("tile", "sec"),
            P("tile", None),
            P("tile", None, None, None),
            P("tile", None, None, None),
            P(),
            P(),
            P(),
            P(),
            P(("sec", "tile"), None, None),
            P(("sec", "tile"), None, None),
            P(),
            P(),
            P(),
            P(),
            P(),
            P(("sec", "tile"), None, None),
            P("tile", "sec", None),
        ),
        out_specs=(
            P(("sec", "tile"), None, None),
            P("tile", "sec", None),
            P(("sec", "tile"), None, None),
            P("tile", "sec", None),
        ),
        check_vma=False,
    )
```

profile of v0, /device:TPU:0, one launch (start us, length us, event | category | flops | bytes accessed | tf_op | source)
XLA Modules:
  0.0 314.4 jit_solution(5274347039851274455)
XLA Ops:
  6.8 7.3 %all-to-all-start = ((f32[32,1,1620]{2,1,0:T(1,128)}), f32[32,1,1620]{2,1,0:T(1,128)S(1)}, u32[]{:S(2)}, u32[]{:S(2)}) async-start(f32[32,1,1620]{2,1,0:T(1,128)} %copy.133), calls=%async_computation | async-start | bytes 425984 | tf_op jit(solution)/shard_map/all_to_all | solution.py:256
  19.8 3.5 %all-to-all-done = f32[32,1,1620]{2,1,0:T(1,128)S(1)} async-done(((f32[32,1,1620]{2,1,0:T(1,128)}), f32[32,1,1620]{2,1,0:T(1,128)S(1)}, u32[]{:S(2)}, u32[]{:S(2)}) %all-to-all-start) | async-done | bytes 207392 | tf_op jit(solution)/shard_map/all_to_all | solution.py:256
  27.9 3.3 %all-to-all-start.1 = ((bf16[32,2,1536]{2,1,0:T(2,128)(2,1)}), bf16[32,2,1536]{2,1,0:T(2,128)(2,1)}, u32[]{:S(2)}, u32[]{:S(2)}) async-start(bf16[32,2,1536]{2,1,0:T(2,128)(2,1)} %reshape.424), calls=%async_computation.1 | async-start | bytes 393216 | tf_op jit(solution)/shard_map/all_to_all | solution.py:243
  42.4 2.8 bitcast_reduce_fusion.1
  52.5 9.1 %all-to-all-start.2 = ((bf16[32,8,384]{2,1,0:T(8,128)(2,1)}), bf16[32,8,384]{2,1,0:T(8,128)(2,1)}, u32[]{:S(2)}, u32[]{:S(2)}) async-start(bf16[32,8,384]{2,1,0:T(8,128)(2,1)} %copy.139), calls=%async_computation.2 | async-start | bytes 393216 | tf_op jit(solution)/shard_map/all_to_all | solution.py:247
  61.6 3.9 %pad_maximum_fusion.narrow = bf16[14,726,128]{2,1,0:T(8,128)(2,1)} fusion(bf16[14,3,128]{2,1,0:T(4,128)(2,1)} %collective-permute-done.3, bf16[3,720,128]{2,1,0:T(8,128)(2,1)S(1)} %collective-permute-done.1, bf16[8,720,128]{2,1,0:T(8,128)(2,1)S(1)} %add_convert_fusion, bf16[3,720,128]{2,1,0:T(8,128)(2,1)S(1)} %collective-permute-done, ...), kind=kLoop, calls=%fused_computation.2 | loop fusion | flops 13009920 | bytes 5203968 | tf_op jit(solution)/shard_map/concatenate | solution.py:18
  68.0 26.0 %shard_map.210 = (bf16[8,720,128]{2,1,0:T(8,128)(2,1)}, f32[8,720,128]{2,1,0:T(8,128)}) custom-call(bf16[14,726,128]{2,1,0:T(8,128)(2,1)} %pad_maximum_fusion.narrow, f32[49,8,128]{2,1,0:T(8,128)} %broadcast_in_dim.26.taps, bf16[8,720,128]{2,1,0:T(8,128)(2,1)} %mul.198.mask, f32[1,128]{1,0:T(1,128)} %get-tuple-element.49.gain, ...), custom_call_target="tpu_custom_call" | custom-call | flops 4494458880 | bytes 4539904 | tf_op jit(solution)/shard_map/pallas_call | solution.py:162
  96.1 2.9 collective-permute-start.4
  121.9 3.4 %reduce.15 = bf16[256,384]{1,0:T(8,128)(2,1)} reduce(bf16[256,1,384]{2,1,0:T(2,128)(2,1)} %bitcast.205, bf16[]{:T(256)} %broadcast.210), dimensions={1}, to_apply=%bitcast.177.reduce_sub_computation | reduce | bytes 393218
  127.0 7.3 %all-to-all-start.3 = ((bf16[32,2,1536]{2,1,0:T(2,128)(2,1)}), bf16[32,2,1536]{2,1,0:T(2,128)(2,1)}, u32[]{:S(2)}, u32[]{:S(2)}) async-start(bf16[32,2,1536]{2,1,0:T(2,128)(2,1)} %reshape.426), calls=%async_computation.3 | async-start | bytes 393216 | tf_op jit(solution)/shard_map/all_to_all | solution.py:243
  137.2 26.0 %shard_map.211 = (bf16[8,720,128]{2,1,0:T(8,128)(2,1)}, f32[8,720,128]{2,1,0:T(8,128)}) custom-call(bf16[14,726,128]{2,1,0:T(8,128)(2,1)} %pad_maximum_fusion.1.narrow, f32[49,8,128]{2,1,0:T(8,128)} %broadcast_in_dim.27.taps, bf16[8,720,128]{2,1,0:T(8,128)(2,1)} %mul.198.mask, f32[1,128]{1,0:T(1,128)} %get-tuple-element.48.gain, ...), custom_call_target="tpu_custom_call" | custom-call | flops 4494458880 | bytes 4539904 | tf_op jit(solution)/shard_map/pallas_call | solution.py:162
  163.1 14.6 %shard_map.212 = bf16[8,720,128]{2,1,0:T(8,128)(2,1)} custom-call(f32[8,720,128]{2,1,0:T(8,128)} %get-tuple-element.12.hidden, bf16[8,720,128]{2,1,0:T(8,128)(2,1)} %cotangent.3, bf16[8,720,128]{2,1,0:T(8,128)(2,1)} %mul.198.mask, f32[1,128]{1,0:T(1,128)} %get-tuple-element.48.gain, bf16[128,512]{1,0:T(8,128)(2,1)} %get-tuple-element.42.expand, ...), custom_call_target="tpu_custom_call" | custom-call | flops 6039797760 | bytes 6291968 | tf_op jit(solution)/shard_map/pallas_call | solution.py:162
  177.7 2.3 fusion.98
  186.0 2.8 bitcast_reduce_fusion
  195.8 9.3 %all-to-all-start.4 = ((bf16[32,8,384]{2,1,0:T(8,128)(2,1)}), bf16[32,8,384]{2,1,0:T(8,128)(2,1)}, u32[]{:S(2)}, u32[]{:S(2)}) async-start(bf16[32,8,384]{2,1,0:T(8,128)(2,1)} %copy.156), calls=%async_computation.4 | async-start | bytes 393216 | tf_op jit(solution)/shard_map/all_to_all | solution.py:247
  205.1 3.2 %pad_maximum_fusion.2.narrow = bf16[14,726,128]{2,1,0:T(8,128)(2,1)} fusion(bf16[14,3,128]{2,1,0:T(4,128)(2,1)S(1)} %collective-permute-done.11, bf16[3,720,128]{2,1,0:T(8,128)(2,1)S(1)} %collective-permute-done.9, bf16[8,720,128]{2,1,0:T(8,128)(2,1)S(1)} %copy-done.1, bf16[3,720,128]{2,1,0:T(8,128)(2,1)S(1)} %collective-permute-done.8, ...), kind=kLoop, calls=%fused_computation.4 | loop fusion | flops 13009920 | bytes 5203968 | tf_op jit(solution)/shard_map/concatenate | solution.py:18
  209.0 30.4 %shard_map.213 = (f32[8,720,128]{2,1,0:T(8,128)}, bf16[8,720,128]{2,1,0:T(8,128)(2,1)}) custom-call(bf16[14,726,128]{2,1,0:T(8,128)(2,1)} %pad_maximum_fusion.2.narrow, f32[49,8,128]{2,1,0:T(8,128)} %broadcast_in_dim.28.taps, bf16[8,720,128]{2,1,0:T(8,128)(2,1)} %cotangent.3, f32[8,720,128]{2,1,0:T(8,128)} %get-tuple-element.13.hidden, ...), custom_call_target="tpu_custom_call" | custom-call | flops 7514357760 | bytes 9094656 | tf_op jit(solution)/shard_map/pallas_call | solution.py:162
  241.6 3.0 collective-permute-start.12
  248.6 7.4 %all-to-all-start.6 = ((f32[32,1,180]{2,1,0:T(1,128)}), f32[32,1,180]{2,1,0:T(1,128)S(1)}, u32[]{:S(2)}, u32[]{:S(2)}) async-start(f32[32,1,180]{2,1,0:T(1,128)} %broadcast_in_dim.31), calls=%async_computation.6 | async-start | bytes 65536 | tf_op jit(solution)/shard_map/all_to_all | solution.py:256
  256.6 6.5 %all-to-all-done.6 = f32[32,1,180]{2,1,0:T(1,128)S(1)} async-done(((f32[32,1,180]{2,1,0:T(1,128)}), f32[32,1,180]{2,1,0:T(1,128)S(1)}, u32[]{:S(2)}, u32[]{:S(2)}) %all-to-all-start.6) | async-done | bytes 23072 | tf_op jit(solution)/shard_map/all_to_all | solution.py:256
  273.3 18.7 %shard_map.214 = f32[8,720,128]{2,1,0:T(8,128)} custom-call(bf16[14,726,128]{2,1,0:T(8,128)(2,1)} %pad_maximum_fusion.3.narrow, f32[49,8,128]{2,1,0:T(8,128)} %broadcast_in_dim.29.taps, f32[8,720,128]{2,1,0:T(8,128)} %get-tuple-element.15.cotangent), custom_call_target="tpu_custom_call" | custom-call | flops 1474560000 | bytes 5751808 | tf_op jit(solution)/shard_map/pallas_call | solution.py:162
  292.0 4.9 %multiply_add_fusion = (f32[8,720,128]{2,1,0:T(8,128)}, f32[8,720,128]{2,1,0:T(8,128)S(1)}) fusion(f32[8,720,128]{2,1,0:T(8,128)} %shard_map.214, f32[128]{0:T(128)S(1)} %copy-done.32, f32[8,720]{1,0:T(8,128)} %multiply_multiply_fusion.2, f32[8,720]{1,0:T(8,128)} %copy-done.14), kind=kLoop, calls=%fused_computation | loop fusion | flops 2211840 | bytes 8893952 | tf_op jit(solution)/shard_map/add | solution.py:470
  297.0 2.9 reduce_sum.38
  302.3 10.7 %all_to_all.51 = f32[32,1,1440]{2,1,0:T(1,128)S(1)} all-to-all(f32[32,1,1440]{2,1,0:T(1,128)S(1)} %copy.160), channel_id=1, replica_groups=mesh['sec'=2,'tile'=16] {'sec','tile'}, dimensions={0} | all-to-all | bytes 368640 | tf_op jit(solution)/shard_map/all_to_all | solution.py:256
  (214 shorter events, 100.8 us)
Async XLA Ops:
  0.6 50.9 %copy-start = (bf16[4,32,32]{2,1,0:T(8,128)(2,1)S(1)}, bf16[4,32,32]{2,1,0:T(8,128)(2,1)}, u32[]{:S(2)}) copy-start(bf16[4,32,32]{2,1,0:T(8,128)(2,1)} %param.30) | copy-start | bytes 24580
  6.8 16.5 %all-to-all-start = ((f32[32,1,1620]{2,1,0:T(1,128)}), f32[32,1,1620]{2,1,0:T(1,128)S(1)}, u32[]{:S(2)}, u32[]{:S(2)}) async-start(f32[32,1,1620]{2,1,0:T(1,128)} %copy.133), calls=%async_computation | async-start | bytes 425984 | tf_op jit(solution)/shard_map/all_to_all | solution.py:256
  27.9 12.2 %all-to-all-start.1 = ((bf16[32,2,1536]{2,1,0:T(2,128)(2,1)}), bf16[32,2,1536]{2,1,0:T(2,128)(2,1)}, u32[]{:S(2)}, u32[]{:S(2)}) async-start(bf16[32,2,1536]{2,1,0:T(2,128)(2,1)} %reshape.424), calls=%async_computation.1 | async-start | bytes 393216 | tf_op jit(solution)/shard_map/all_to_all | solution.py:243
  35.9 12.9 %collective-permute-start = (bf16[3,720,128]{2,1,0:T(8,128)(2,1)}, bf16[3,720,128]{2,1,0:T(8,128)(2,1)S(1)}, u32[]{:S(2)}, u32[]{:S(2)}) collective-permute-start(bf16[3,720,128]{2,1,0:T(8,128)(2,1)} %get-tuple-element.34), channel_id=1, source_target_pairs={{0,1},{1,2},{2,3},{3,4},{4,5},{5,6},{6,7},{7,8},{8,9},{9,10},{10,1... | collective-permute-start | bytes 1658888 | tf_op jit(solution)/shard_map/ppermute | solution.py:16
  38.2 10.7 %collective-permute-start.1 = (bf16[3,720,128]{2,1,0:T(8,128)(2,1)}, bf16[3,720,128]{2,1,0:T(8,128)(2,1)S(1)}, u32[]{:S(2)}, u32[]{:S(2)}) collective-permute-start(bf16[3,720,128]{2,1,0:T(8,128)(2,1)} %get-tuple-element.35), channel_id=1, source_target_pairs={{1,0},{2,1},{3,2},{4,3},{5,4},{6,5},{7,6},{8,7},{9,8},{10,9},{11,1... | collective-permute-start | bytes 1658888 | tf_op jit(solution)/shard_map/ppermute | solution.py:17
  49.5 12.1 %collective-permute-start.2 = (bf16[14,3,128]{2,1,0:T(4,128)(2,1)}, bf16[14,3,128]{2,1,0:T(4,128)(2,1)}, u32[]{:S(2)}, u32[]{:S(2)}) collective-permute-start(bf16[14,3,128]{2,1,0:T(4,128)(2,1)} %get-tuple-element.26), channel_id=1, source_target_pairs={{0,16},{16,0},{1,17},{17,1},{2,18},{18,2},{3,19},{19,3},{4,20},{20... | collective-permute-start | bytes 32264 | tf_op jit(solution)/shard_map/ppermute | solution.py:16
  50.5 11.1 %collective-permute-start.3 = (bf16[14,3,128]{2,1,0:T(4,128)(2,1)}, bf16[14,3,128]{2,1,0:T(4,128)(2,1)}, u32[]{:S(2)}, u32[]{:S(2)}) collective-permute-start(bf16[14,3,128]{2,1,0:T(4,128)(2,1)} %get-tuple-element.27), channel_id=1, source_target_pairs={{16,0},{0,16},{17,1},{1,17},{18,2},{2,18},{19,3},{3,19},{20,4},{4,... | collective-permute-start | bytes 32264 | tf_op jit(solution)/shard_map/ppermute | solution.py:17
  52.5 58.4 %all-to-all-start.2 = ((bf16[32,8,384]{2,1,0:T(8,128)(2,1)}), bf16[32,8,384]{2,1,0:T(8,128)(2,1)}, u32[]{:S(2)}, u32[]{:S(2)}) async-start(bf16[32,8,384]{2,1,0:T(8,128)(2,1)} %copy.139), calls=%async_computation.2 | async-start | bytes 393216 | tf_op jit(solution)/shard_map/all_to_all | solution.py:247
  96.1 17.1 %collective-permute-start.4 = (bf16[3,720,128]{2,1,0:T(8,128)(2,1)}, bf16[3,720,128]{2,1,0:T(8,128)(2,1)}, u32[]{:S(2)}, u32[]{:S(2)}) collective-permute-start(bf16[3,720,128]{2,1,0:T(8,128)(2,1)} %get-tuple-element.33), channel_id=1, source_target_pairs={{0,1},{1,2},{2,3},{3,4},{4,5},{5,6},{6,7},{7,8},{8,9},{9,10},{10,1... | collective-permute-start | bytes 1658888 | tf_op jit(solution)/shard_map/ppermute | solution.py:16
  98.9 15.6 %collective-permute-start.5 = (bf16[3,720,128]{2,1,0:T(8,128)(2,1)S(1)}, bf16[3,720,128]{2,1,0:T(8,128)(2,1)S(1)}, u32[]{:S(2)}, u32[]{:S(2)}) collective-permute-start(bf16[3,720,128]{2,1,0:T(8,128)(2,1)S(1)} %get-tuple-element.32), channel_id=1, source_target_pairs={{1,0},{2,1},{3,2},{4,3},{5,4},{6,5},{7,6},{8,7},{9,8},{10,9},{11,1... | collective-permute-start | bytes 1658888 | tf_op jit(solution)/shard_map/ppermute | solution.py:17
  116.7 17.6 %collective-permute-start.6 = (bf16[14,3,128]{2,1,0:T(4,128)(2,1)}, bf16[14,3,128]{2,1,0:T(4,128)(2,1)S(1)}, u32[]{:S(2)}, u32[]{:S(2)}) collective-permute-start(bf16[14,3,128]{2,1,0:T(4,128)(2,1)} %get-tuple-element.24), channel_id=1, source_target_pairs={{0,16},{16,0},{1,17},{17,1},{2,18},{18,2},{3,19},{19,3},{4,20},{20... | collective-permute-start | bytes 32264 | tf_op jit(solution)/shard_map/ppermute | solution.py:16
  118.3 15.9 %collective-permute-start.7 = (bf16[14,3,128]{2,1,0:T(4,128)(2,1)}, bf16[14,3,128]{2,1,0:T(4,128)(2,1)S(1)}, u32[]{:S(2)}, u32[]{:S(2)}) collective-permute-start(bf16[14,3,128]{2,1,0:T(4,128)(2,1)} %get-tuple-element.25), channel_id=1, source_target_pairs={{16,0},{0,16},{17,1},{1,17},{18,2},{2,18},{19,3},{3,19},{20,4},{4,... | collective-permute-start | bytes 32264 | tf_op jit(solution)/shard_map/ppermute | solution.py:17
  127.0 56.8 %all-to-all-start.3 = ((bf16[32,2,1536]{2,1,0:T(2,128)(2,1)}), bf16[32,2,1536]{2,1,0:T(2,128)(2,1)}, u32[]{:S(2)}, u32[]{:S(2)}) async-start(bf16[32,2,1536]{2,1,0:T(2,128)(2,1)} %reshape.426), calls=%async_computation.3 | async-start | bytes 393216 | tf_op jit(solution)/shard_map/all_to_all | solution.py:243
  180.0 12.7 %collective-permute-start.8 = (bf16[3,720,128]{2,1,0:T(8,128)(2,1)}, bf16[3,720,128]{2,1,0:T(8,128)(2,1)S(1)}, u32[]{:S(2)}, u32[]{:S(2)}) collective-permute-start(bf16[3,720,128]{2,1,0:T(8,128)(2,1)} %get-tuple-element.30), channel_id=1, source_target_pairs={{0,1},{1,2},{2,3},{3,4},{4,5},{5,6},{6,7},{7,8},{8,9},{9,10},{10,1... | collective-permute-start | bytes 1658888 | tf_op jit(solution)/shard_map/ppermute | solution.py:16
  182.3 10.4 %collective-permute-start.9 = (bf16[3,720,128]{2,1,0:T(8,128)(2,1)}, bf16[3,720,128]{2,1,0:T(8,128)(2,1)S(1)}, u32[]{:S(2)}, u32[]{:S(2)}) collective-permute-start(bf16[3,720,128]{2,1,0:T(8,128)(2,1)} %get-tuple-element.31), channel_id=1, source_target_pairs={{1,0},{2,1},{3,2},{4,3},{5,4},{6,5},{7,6},{8,7},{9,8},{10,9},{11,1... | collective-permute-start | bytes 1658888 | tf_op jit(solution)/shard_map/ppermute | solution.py:17
  192.7 12.4 %collective-permute-start.10 = (bf16[14,3,128]{2,1,0:T(4,128)(2,1)S(1)}, bf16[14,3,128]{2,1,0:T(4,128)(2,1)S(1)}, u32[]{:S(2)}, u32[]{:S(2)}) collective-permute-start(bf16[14,3,128]{2,1,0:T(4,128)(2,1)S(1)} %get-tuple-element.22), channel_id=1, source_target_pairs={{0,16},{16,0},{1,17},{17,1},{2,18},{18,2},{3,19},{19,3},{4,20},{20... | collective-permute-start | bytes 32264 | tf_op jit(solution)/shard_map/ppermute | solution.py:16
  194.4 10.7 %collective-permute-start.11 = (bf16[14,3,128]{2,1,0:T(4,128)(2,1)S(1)}, bf16[14,3,128]{2,1,0:T(4,128)(2,1)S(1)}, u32[]{:S(2)}, u32[]{:S(2)}) collective-permute-start(bf16[14,3,128]{2,1,0:T(4,128)(2,1)S(1)} %get-tuple-element.23), channel_id=1, source_target_pairs={{16,0},{0,16},{17,1},{1,17},{18,2},{2,18},{19,3},{3,19},{20,4},{4,... | collective-permute-start | bytes 32264 | tf_op jit(solution)/shard_map/ppermute | solution.py:17
  195.8 48.8 %all-to-all-start.4 = ((bf16[32,8,384]{2,1,0:T(8,128)(2,1)}), bf16[32,8,384]{2,1,0:T(8,128)(2,1)}, u32[]{:S(2)}, u32[]{:S(2)}) async-start(bf16[32,8,384]{2,1,0:T(8,128)(2,1)} %copy.156), calls=%async_computation.4 | async-start | bytes 393216 | tf_op jit(solution)/shard_map/all_to_all | solution.py:247
  209.0 35.6 %copy-start.10 = (bf16[1,360,384]{2,1,0:T(8,128)(2,1)S(1)}, bf16[1,360,384]{2,1,0:T(8,128)(2,1)}, u32[]{:S(2)}) copy-start(bf16[1,360,384]{2,1,0:T(8,128)(2,1)} %param.36) | copy-start | bytes 829444
  241.6 22.0 %collective-permute-start.12 = (bf16[3,720,128]{2,1,0:T(8,128)(2,1)}, bf16[3,720,128]{2,1,0:T(8,128)(2,1)}, u32[]{:S(2)}, u32[]{:S(2)}) collective-permute-start(bf16[3,720,128]{2,1,0:T(8,128)(2,1)} %get-tuple-element.29), channel_id=1, source_target_pairs={{0,1},{1,2},{2,3},{3,4},{4,5},{5,6},{6,7},{7,8},{8,9},{9,10},{10,1... | collective-permute-start | bytes 1658888 | tf_op jit(solution)/shard_map/ppermute | solution.py:16
  245.9 19.0 %collective-permute-start.13 = (bf16[3,720,128]{2,1,0:T(8,128)(2,1)S(1)}, bf16[3,720,128]{2,1,0:T(8,128)(2,1)}, u32[]{:S(2)}, u32[]{:S(2)}) collective-permute-start(bf16[3,720,128]{2,1,0:T(8,128)(2,1)S(1)} %get-tuple-element.28), channel_id=1, source_target_pairs={{1,0},{2,1},{3,2},{4,3},{5,4},{6,5},{7,6},{8,7},{9,8},{10,9},{11,1... | collective-permute-start | bytes 1658888 | tf_op jit(solution)/shard_map/ppermute | solution.py:17
  248.6 14.4 %all-to-all-start.6 = ((f32[32,1,180]{2,1,0:T(1,128)}), f32[32,1,180]{2,1,0:T(1,128)S(1)}, u32[]{:S(2)}, u32[]{:S(2)}) async-start(f32[32,1,180]{2,1,0:T(1,128)} %broadcast_in_dim.31), calls=%async_computation.6 | async-start | bytes 65536 | tf_op jit(solution)/shard_map/all_to_all | solution.py:256
  266.1 3.8 %collective-permute-start.14 = (bf16[14,3,128]{2,1,0:T(4,128)(2,1)S(1)}, bf16[14,3,128]{2,1,0:T(4,128)(2,1)S(1)}, u32[]{:S(2)}, u32[]{:S(2)}) collective-permute-start(bf16[14,3,128]{2,1,0:T(4,128)(2,1)S(1)} %get-tuple-element.20), channel_id=1, source_target_pairs={{0,16},{16,0},{1,17},{17,1},{2,18},{18,2},{3,19},{19,3},{4,20},{20... | collective-permute-start | bytes 32264 | tf_op jit(solution)/shard_map/ppermute | solution.py:16
  266.8 3.7 %collective-permute-start.15 = (bf16[14,3,128]{2,1,0:T(4,128)(2,1)S(1)}, bf16[14,3,128]{2,1,0:T(4,128)(2,1)S(1)}, u32[]{:S(2)}, u32[]{:S(2)}) collective-permute-start(bf16[14,3,128]{2,1,0:T(4,128)(2,1)S(1)} %get-tuple-element.21), channel_id=1, source_target_pairs={{16,0},{0,16},{17,1},{1,17},{18,2},{2,18},{19,3},{3,19},{20,4},{4,... | collective-permute-start | bytes 32264 | tf_op jit(solution)/shard_map/ppermute | solution.py:17
  (34 other events, 377.8 us)
where the time goes:
time: 316 us; the launch traced here: 314 us
  Pallas kernels  116 us (37%)
  starting transfers between devices  67.7 us (21%)
  local copies, waits for them, and re-layouts  55.2 us (17%)
  other arithmetic  31.4 us (10%)
  matrix products  19.9 us (6%)
  waiting for transfers between devices  12.4 us (4%)
  blocking collectives  10.7 us (3%)
    pallas_call x5, Pallas kernels, run_kernel(): pl.pallas_call(kernel, out_shape=outs, in_specs=[pl.BlockSpec(memory_spac...  116 us
    unnamed x88, local copies, waits for them, and re-layouts  18.7 us
    all_to_all x2, starting transfers between devices, to_bands(): lax.all_to_all(values, ('sec', 'tile'), split_axis=0, concat_axis=1, tile...  18.4 us
    ppermute x8, starting transfers between devices, with_halo(): before = lax.ppermute(last, axis, up)  15.4 us
    all_to_all x2, starting transfers between devices, swap(): lax.all_to_all(values, ('sec', 'tile'), split_axis=0, concat_axis=0, tile...  14.7 us
    concatenate x4, other arithmetic, with_halo(): x = jnp.concatenate([before, x, after], axis=dim)  11.4 us
    all_to_all x1, blocking collectives, swap(): lax.all_to_all(values, ('sec', 'tile'), split_axis=0, concat_axis=0, tile...  10.7 us
    all_to_all x2, starting transfers between devices, to_modes(): lax.all_to_all(values, ('sec', 'tile'), split_axis=1, concat_axis=0, tile...  10.6 us
  transfers between devices with their start and end apart: 22, of which 5 were waited for; matrix products, arithmetic and copies ran while one was open for 25% of the time, Pallas kernels for 31%

commit v1 on v0

v1 whole, which is shorter than its diff:
```python
import functools

import jax
import jax.numpy as jnp
import numpy as np
from jax import lax
from jax.experimental import pallas as pl
from jax.experimental.pallas import tpu as pltpu
from jax.sharding import PartitionSpec as P

MESH = pl.DeviceIdType.MESH
F32 = jnp.float32
BF16 = jnp.bfloat16
GELU_SCALE = 0.7978845608028654
GELU_CUBIC = 0.044715
EPSILON = 1e-06
MARGIN = 16
SLOTS = 8
LANES = 128


def wave_table(lon_count, mode_count):
    longitude = np.arange(lon_count)
    wavenumber = np.arange(mode_count)
    phase = (longitude[:, None] * wavenumber[None, :] % lon_count) * (2.0 * np.pi / lon_count)
    scaled = np.stack([np.cos(phase), -np.sin(phase)], axis=2) * np.sqrt(2.0 / lon_count)
    return scaled.reshape(lon_count, 2 * mode_count).astype(np.float32).astype(BF16)


def mode_order(lat_count, modes):
    source = np.arange(lat_count * modes * 2)
    lat, mode, part = source // (2 * modes), source % (2 * modes) // 2, source % 2
    matrix = np.zeros((source.size, source.size), np.float32)
    matrix[(part * modes + mode) * lat_count + lat, source] = 1.0
    return matrix.astype(BF16)


def dot(a, b):
    return lax.dot_general(a, b, (((1,), (0,)), ((), ())), preferred_element_type=F32)


def dot_nt(a, b):
    return lax.dot_general(a, b, (((1,), (1,)), ((), ())), preferred_element_type=F32)


def dot_tn(a, b):
    return lax.dot_general(a, b, (((0,), (0,)), ((), ())), preferred_element_type=F32)


def halves(x):
    high = x.astype(BF16)
    return high, (x - high.astype(F32)).astype(BF16)


def loop(count, body):
    def step(index, carry):
        body(index)
        return carry

    lax.fori_loop(0, count, step, jnp.int32(0))


def normalize(hidden):
    center = hidden - jnp.mean(hidden, axis=-1, keepdims=True)
    inverse_std = lax.rsqrt(jnp.mean(center * center, axis=-1, keepdims=True) + EPSILON)
    return center * inverse_std, inverse_std


def gelu_parts(before):
    square = before * before
    wave = jnp.tanh(before * (GELU_SCALE + (GELU_SCALE * GELU_CUBIC) * square))
    return square, wave


def gelu_value(before, wave):
    scaled = 0.5 * before
    return scaled + scaled * wave


def gelu_slope(before, square, wave):
    slope = (0.5 * GELU_SCALE + (1.5 * GELU_SCALE * GELU_CUBIC) * square) * before
    return 0.5 + 0.5 * wave + slope * (1.0 - wave * wave)


def window_kernel(
    axes,
    atm, ocean, mask, bands, oreg, areg, read, embed, flux_read_t, flux_embed,
    leg_f, leg_i, smix, taps_in, gains, expand, project, acot, ocot,
    table, table_t, order, order_t,
    atm_next, ocean_next, atm_grad, ocean_grad,
    win, wide, hid, taps, mask_wide, repeat, surf, gall, fold,
    wo, wa, flux_send, flux_recv, cp_send, cp_recv, sa_send, sa_recv, fa_send, fa_recv,
    xs, xr, flat, mixed, spec_a, spec_b,
    halo_send, halo_recv, x_send, x_recv, near_send, near_recv,
):
    sections, tiles = axes
    devices = sections * tiles
    sec = lax.axis_index("sec")
    tile = lax.axis_index("tile")
    me = sec * tiles + tile
    rows, extent, channels = ocean.shape
    lon = atm.shape[0]
    radius = (win.shape[1] - rows) // 2
    side = 2 * radius + 1
    part = lon // sections
    ratio = extent // part
    cols = xs.shape[2]
    right = MARGIN + extent

    def target(device):
        return {"sec": lax.div(device, tiles), "tile": lax.rem(device, tiles)}

    barrier = pltpu.get_barrier_semaphore()

    def greet(step):
        pl.semaphore_signal(
            barrier, inc=1, device_id=target(lax.rem(me + 1 + step, devices)), device_id_type=MESH
        )

    loop(devices - 1, greet)

    @pl.when(tile == 0)
    def _():
        win[:, 0:radius] = jnp.zeros((win.shape[0], radius) + win.shape[2:], BF16)

    @pl.when(tile == tiles - 1)
    def _():
        win[:, radius + rows :] = jnp.zeros((win.shape[0], radius) + win.shape[2:], BF16)

    x_index = lax.broadcasted_iota(jnp.int32, (extent, lon), 0)
    g_index = lax.broadcasted_iota(jnp.int32, (extent, lon), 1)
    offset = x_index - (g_index - sec * part) * ratio
    repeat[...] = jnp.where((offset >= 0) & (offset < ratio), 1.0, 0.0).astype(BF16)

    for row in range(rows):
        surf[row : row + 1, :] = dot_nt(read[...], ocean[row])
    mask_value = mask[...].astype(F32)
    high, low = halves(surf[...] * mask_value * (1.0 / ratio))
    surf[:, 0:lon] = dot(high, repeat[...]) + dot(low, repeat[...])

    flux_send[...] = dot_nt(flux_read_t[...], atm[...])

    def weights(slot):
        band = lax.rem(2 * tile - 2 + slot + devices, devices)
        for row in range(rows):
            to_ocean = jnp.float32(0.0)
            to_atm = jnp.float32(0.0)
            for peer in range(bands.shape[1]):
                same = jnp.where(bands[0, peer] == band, 1.0, 0.0)
                to_ocean = to_ocean + same * oreg[peer, row]
                to_atm = to_atm + same * areg[peer, row]
            wo[slot, row] = to_ocean
            wa[slot, row] = to_atm

    loop(SLOTS, weights)

    def coarse_part(slot):
        total = wa[slot, 0] * surf[0:1, 0:lon]
        for row in range(1, rows):
            total = total + wa[slot, row] * surf[row : row + 1, 0:lon]
        cp_send[slot] = total

    loop(SLOTS, coarse_part)

    pl.semaphore_wait(barrier, devices - 1)

    def band_to_groups(index, source, slots, act):
        def one(step):
            turn, section = lax.div(step, sections), lax.rem(step, sections)
            group = lax.rem(lax.div(me, 2) + 1 - turn + tiles, tiles)
            slot = lax.rem(me, 2) + 2 * turn
            away = (section != sec) | (group != tile)

            def remote():
                return pltpu.make_async_remote_copy(
                    src_ref=source,
                    dst_ref=slots.at[slot],
                    send_sem=near_send.at[index, step],
                    recv_sem=near_recv.at[index],
                    device_id={"sec": section, "tile": group},
                    device_id_type=MESH,
                )

            @pl.when(away)
            def _():
                act(remote())

            if act is start:

                @pl.when(jnp.logical_not(away))
                def _():
                    pltpu.make_async_copy(source, slots.at[slot], near_recv.at[index]).start()

        loop(SLOTS // 2 * sections, one)

    def group_to_bands(index, parts, slots, act):
        def one(slot):
            band = lax.rem(2 * tile - 2 + slot + devices, devices)
            place = lax.div(slot, 2) * sections + sec

            def remote():
                return pltpu.make_async_remote_copy(
                    src_ref=parts.at[slot],
                    dst_ref=slots.at[place],
                    send_sem=near_send.at[index, slot],
                    recv_sem=near_recv.at[index],
                    device_id=target(band),
                    device_id_type=MESH,
                )

            @pl.when(band != me)
            def _():
                act(remote())

            if act is start:

                @pl.when(band == me)
                def _():
                    pltpu.make_async_copy(
                        parts.at[slot], slots.at[place], near_recv.at[index]
                    ).start()

        loop(SLOTS, one)

    def start(copy):
        copy.start()

    def sent(copy):
        copy.wait_send()

    def near_wait(index, slots):
        pltpu.make_async_copy(slots, slots, near_recv.at[index]).wait()

    def all_start(index):
        pltpu.make_async_copy(xs.at[index, me], xr.at[index, me], x_recv.at[index]).start()

        def one(step):
            peer = lax.rem(me + 1 + step, devices)
            pltpu.make_async_remote_copy(
                src_ref=xs.at[index, peer],
                dst_ref=xr.at[index, me],
                send_sem=x_send.at[index],
                recv_sem=x_recv.at[index],
                device_id=target(peer),
                device_id_type=MESH,
            ).start()

        loop(devices - 1, one)

    def all_wait(index):
        pltpu.make_async_copy(xr.at[index], xr.at[index], x_recv.at[index]).wait()

    def all_sent(index):
        others = xs.at[index, pl.ds(0, devices - 1)]
        pltpu.make_async_copy(others, others, x_send.at[index]).wait()

    def rim(layer, row_step, col_step):
        number = (row_step + 1) * 3 + col_step + 1
        number = number if number < 4 else number - 1
        source_rows = {-1: (radius, radius), 0: (radius, rows), 1: (rows, radius)}[row_step]
        place_rows = {-1: (radius + rows, radius), 0: (radius, rows), 1: (0, radius)}[row_step]
        inner = {-1: (MARGIN, MARGIN), 0: (MARGIN, extent), 1: (extent, MARGIN)}[col_step]
        outer = {-1: (right, MARGIN), 0: (MARGIN, extent), 1: (0, MARGIN)}[col_step]
        return pltpu.make_async_remote_copy(
            src_ref=win.at[layer, pl.ds(*source_rows), pl.ds(*inner)],
            dst_ref=win.at[layer, pl.ds(*place_rows), pl.ds(*outer)],
            send_sem=halo_send.at[layer, number],
            recv_sem=halo_recv.at[layer, number],
            device_id={
                "sec": lax.rem(sec + col_step + sections, sections),
                "tile": lax.rem(tile + row_step + tiles, tiles),
            },
            device_id_type=MESH,
        )

    def rims(layer, act, sending, row_steps):
        for row_step in row_steps:
            edge = {-1: 0, 0: None, 1: tiles - 1}[row_step if sending else -row_step]

            def each(row_step=row_step):
                for col_step in (0, -1, 1):
                    if (row_step, col_step) != (0, 0):
                        act(rim(layer, row_step, col_step))

            if edge is None:
                each()
            else:
                pl.when(tile != edge)(each)

    def rims_start(layer):
        rims(layer, lambda copy: copy.start(), True, (0, -1, 1))

    def rims_sent(layer):
        rims(layer, lambda copy: copy.wait_send(), True, (0, -1, 1))

    def rims_wait(layer, row_steps):
        rims(layer, lambda copy: copy.wait_recv(), False, row_steps)

    def widen(layer, first, count):
        def one(index):
            wide[first + index] = win[layer, first + index].astype(F32)

        loop(count, one)

    def depthwise(kernel, flip, lines, base, store):
        def step(index):
            begin = pl.multiple_of(index * 8, 8)
            totals = [None] * rows
            for col in range(side):
                tap = [
                    taps[kernel, side * side - 1 - (u * side + col) if flip else u * side + col]
                    for u in range(side)
                ]
                for line in lines:
                    piece = wide[line, pl.ds(begin + (MARGIN - radius + col), 8), :]
                    for u in range(side):
                        place = line - u
                        if 0 <= place < rows:
                            term = piece * tap[u]
                            old = totals[place]
                            totals[place] = term if old is None else old + term
            for row in range(rows):
                if totals[row] is not None:
                    before = base(row, begin)
                    store(row, begin, totals[row] if before is None else before + totals[row])

        loop(extent // 8, step)

    own_lines = range(radius, radius + rows)
    rim_lines = list(range(radius)) + list(range(radius + rows, rows + 2 * radius))

    def first_part(layer, kernel, flip, base, store):
        rims_wait(layer, (0,))
        widen(layer, radius, rows)
        depthwise(kernel, flip, own_lines, base, store)

    def second_part(layer, kernel, flip, base, store):
        rims_wait(layer, (-1, 1))
        widen(layer, 0, radius)
        widen(layer, radius + rows, radius)
        depthwise(kernel, flip, rim_lines, base, store)

    height = max(cols, 8)
    group = height // cols

    def unpack(index):
        def one(block):
            pieces = [
                xr[index, block * group + place].astype(F32) for place in range(group)
            ]
            flat[pl.ds(pl.multiple_of(block * height, height), height), :] = (
                pieces[0] if group == 1 else jnp.concatenate(pieces, axis=0)
            )

        loop(devices // group, one)
        return flat[...].astype(BF16)

    def pack(index, value):
        flat[...] = value

        def one(block):
            piece = flat[pl.ds(pl.multiple_of(block * height, height), height), :].astype(BF16)
            for place in range(group):
                xs[index, block * group + place] = piece[place * cols : (place + 1) * cols]

        loop(devices // group, one)
        all_start(index)

    def spectral(index, first, first_dot, second, second_dot, adjoint):
        modes, lat = first.shape[0], first.shape[1]
        half = modes * lat
        all_wait(index)
        spec_a[...] = dot(order[...], unpack(index)).astype(BF16)
        for block in range(2 * modes):
            piece = pl.ds(block * lat, lat)
            spec_b[piece] = first_dot(first[block % modes], spec_a[piece]).astype(BF16)
        real, imag = spec_b[0:half], spec_b[half : 2 * half]
        if adjoint:
            spec_a[0:half] = (dot_nt(real, smix[0]) + dot_nt(imag, smix[1])).astype(BF16)
            spec_a[half : 2 * half] = (dot_nt(imag, smix[0]) - dot_nt(real, smix[1])).astype(BF16)
        else:
            spec_a[0:half] = (dot(real, smix[0]) - dot(imag, smix[1])).astype(BF16)
            spec_a[half : 2 * half] = (dot(imag, smix[0]) + dot(real, smix[1])).astype(BF16)
        for block in range(2 * modes):
            piece = pl.ds(block * lat, lat)
            spec_b[piece] = second_dot(second[block % modes], spec_a[piece]).astype(BF16)
        pack(index + 1, dot(order_t[...], spec_b[...]))

    band_to_groups(0, flux_send, flux_recv, start)
    group_to_bands(1, cp_send, cp_recv, start)

    lane_row = lax.broadcasted_iota(jnp.int32, (rows, rows * LANES), 1)
    sub_row = lax.broadcasted_iota(jnp.int32, (rows, rows * LANES), 0)
    inside = (lane_row >= sub_row * LANES) & (lane_row < (sub_row + 1) * LANES)
    spread = jnp.where(inside, 1.0, 0.0).astype(BF16)
    column = dot_tn(mask_value.astype(BF16), spread)
    for row in range(rows):
        mask_wide[row] = column[:, row * LANES : (row + 1) * LANES].astype(BF16)

    def tap_tile(index):
        for kernel in range(taps.shape[0]):
            taps[kernel, index] = jnp.broadcast_to(
                taps_in[kernel, pl.ds(index, 1), :], (8, channels)
            )

    loop(side * side, tap_tile)

    near_wait(0, flux_recv)
    for row in range(rows):
        total = wo[0, row] * flux_recv[0]
        for slot in range(1, SLOTS):
            total = total + wo[slot, row] * flux_recv[slot]
        high, low = halves(total)
        embed_rows = flux_embed[...]
        gall[row] = (dot_tn(high, embed_rows) + dot_tn(low, embed_rows)).astype(BF16)

    def force(row):
        forcing = dot(repeat[...], gall[row])
        state = ocean[row].astype(F32) + mask_wide[row].astype(F32) * forcing
        win[0, row + radius, MARGIN:right, :] = state.astype(BF16)

    loop(rows, force)
    rims_start(0)

    near_wait(1, cp_recv)
    total = cp_recv[0]
    for slot in range(1, SLOTS // 2 * sections):
        total = total + cp_recv[slot]
    high, low = halves(total)
    embed_high, embed_low = halves(embed[...])
    outer = dot_tn(
        jnp.concatenate([high, low, high], axis=0),
        jnp.concatenate([embed_high, embed_high, embed_low], axis=0),
    )
    mixed[...] = (atm[...].astype(F32) + outer).astype(BF16)
    pack(0, dot(table_t[...], mixed[...]))

    def forward_cells(layer, store):
        def cells(row):
            unit, _ = normalize(hid[layer, row])
            normed = (unit * gains[layer : layer + 1, :]).astype(BF16)
            before = dot(normed, expand[layer])
            _, wave = gelu_parts(before)
            active = gelu_value(before, wave).astype(BF16)
            update = dot(active, project[layer])
            old = wide[row + radius, MARGIN:right, :]
            store(row, (old + mask_wide[row].astype(F32) * update).astype(BF16))

        loop(rows, cells)

    def hidden_store(layer):
        def store(row, begin, value):
            hid[layer, row, pl.ds(begin, 8), :] = value

        return store

    def hidden_base(layer):
        return lambda row, begin: hid[layer, row, pl.ds(begin, 8), :]

    nothing = lambda row, begin: None

    first_part(0, 0, False, nothing, hidden_store(0))
    spectral(0, leg_f, dot, leg_i, dot, False)
    second_part(0, 0, False, hidden_base(0), hidden_store(0))

    def to_window(row, value):
        win[1, row + radius, MARGIN:right, :] = value

    forward_cells(0, to_window)
    rims_start(1)

    all_wait(1)
    response = dot(table[...], unpack(1))
    square, wave = gelu_parts(response)
    atm_next[...] = (mixed[...].astype(F32) + gelu_value(response, wave)).astype(BF16)
    slope = gelu_slope(response, square, wave)
    mixed[...] = (slope * acot[...].astype(F32)).astype(BF16)
    pack(2, dot(table_t[...], mixed[...]))

    first_part(1, 1, False, nothing, hidden_store(1))
    spectral(2, leg_i, dot_tn, leg_f, dot_tn, True)
    second_part(1, 1, False, hidden_base(1), hidden_store(1))

    def backward(layer, row, hidden, cotangent, window):
        gain = gains[layer : layer + 1, :]
        unit, inverse_std = normalize(hidden)
        normed = (unit * gain).astype(BF16)
        before = dot(normed, expand[layer])
        masked = (mask_wide[row].astype(F32) * cotangent).astype(BF16)
        active_adjoint = dot_nt(masked, project[layer])
        square, wave = gelu_parts(before)
        before_adjoint = (gelu_slope(before, square, wave) * active_adjoint).astype(BF16)
        scaled = dot_nt(before_adjoint, expand[layer]) * gain
        adjoint = inverse_std * (
            scaled
            - jnp.mean(scaled, axis=-1, keepdims=True)
            - unit * jnp.mean(scaled * unit, axis=-1, keepdims=True)
        )
        win[window, row + radius, MARGIN:right, :] = adjoint.astype(BF16)
        return before, wave

    def turn(row):
        before, wave = backward(1, row, hid[1, row], ocot[row].astype(F32), 2)
        active = gelu_value(before, wave).astype(BF16)
        update = dot(active, project[1])
        old = wide[row + radius, MARGIN:right, :]
        ocean_next[row] = (old + mask_wide[row].astype(F32) * update).astype(BF16)

    loop(rows, turn)
    rims_start(2)

    all_wait(3)
    acot_wide = acot[...].astype(F32)
    input_adjoint = acot_wide + dot(table[...], unpack(3))
    atm_grad[...] = input_adjoint
    high, low = halves(input_adjoint)
    embed_high, embed_low = halves(embed[...])
    sa_send[...] = (
        dot_nt(embed_high, high) + dot_nt(embed_low, high) + dot_nt(embed_high, low)
    )
    band_to_groups(2, sa_send, sa_recv, start)

    def grad_store(row, begin, value):
        ocean_grad[row, pl.ds(begin, 8), :] = value

    def grad_base(row, begin):
        return ocean_grad[row, pl.ds(begin, 8), :]

    def given(row, begin):
        return ocot[row, pl.ds(begin, 8), :].astype(F32)

    first_part(2, 1, True, given, grad_store)
    second_part(2, 1, True, grad_base, grad_store)

    loop(rows, lambda row: backward(0, row, hid[0, row], ocean_grad[row], 3) and None)
    rims_start(3)

    near_wait(2, sa_recv)
    for row in range(rows):
        total = wa[0, row] * sa_recv[0]
        for slot in range(1, SLOTS):
            total = total + wa[slot, row] * sa_recv[slot]
        surf[row : row + 1, 0:lon] = total
    high, low = halves(surf[:, 0:lon])
    widened = (dot_nt(high, repeat[...]) + dot_nt(low, repeat[...])) * mask_value * (1.0 / ratio)
    surf[...] = widened

    first_part(3, 0, True, grad_base, grad_store)
    second_part(3, 0, True, grad_base, grad_store)

    def fold_row(row):
        masked = (mask_wide[row].astype(F32) * ocean_grad[row]).astype(BF16)
        fold[row] = dot_nt(flux_embed[...], masked)

    loop(rows, fold_row)
    for row in range(rows):
        high, low = halves(fold[row])
        fold[row, :, 0:lon] = dot(high, repeat[...]) + dot(low, repeat[...])

    def flux_part(slot):
        total = wo[slot, 0] * fold[0, :, 0:lon]
        for row in range(1, rows):
            total = total + wo[slot, row] * fold[row, :, 0:lon]
        fa_send[slot] = total

    loop(SLOTS, flux_part)
    group_to_bands(3, fa_send, fa_recv, start)

    read_rows = jnp.concatenate([read[...].astype(F32)] * rows, axis=1)
    block_read = jnp.where(inside, read_rows, 0.0).astype(BF16)
    high, low = halves(surf[...])
    share = dot_tn(high, block_read) + dot_tn(low, block_read)
    for row in range(rows):
        ocean_grad[row] = ocean_grad[row] + share[:, row * LANES : (row + 1) * LANES]

    near_wait(3, fa_recv)
    total = fa_recv[0]
    for slot in range(1, SLOTS // 2 * sections):
        total = total + fa_recv[slot]
    high, low = halves(total)
    rows_read = flux_read_t[...]
    atm_grad[...] = atm_grad[...] + dot_tn(high, rows_read) + dot_tn(low, rows_read)

    band_to_groups(0, flux_send, flux_recv, sent)
    group_to_bands(1, cp_send, cp_recv, sent)
    band_to_groups(2, sa_send, sa_recv, sent)
    group_to_bands(3, fa_send, fa_recv, sent)
    for index in range(xs.shape[0]):
        all_sent(index)
    for layer in range(win.shape[0]):
        rims_sent(layer)


def per_device(
    atmosphere,
    ocean_state,
    land_mask,
    crossing_bands,
    ocean_regrid,
    atmosphere_regrid,
    surface_read,
    surface_embed,
    flux_read,
    flux_embed,
    legendre_forward,
    legendre_inverse,
    spectral_mix,
    conv_kernel,
    norm_gain,
    expand_weight,
    project_weight,
    atmosphere_cotangent,
    ocean_cotangent,
):
    axes = (lax.axis_size("sec"), lax.axis_size("tile"))
    devices = axes[0] * axes[1]
    lat_rows, lon, channels = atmosphere.shape
    rows, extent, ocean_channels = ocean_state.shape
    layers, side = conv_kernel.shape[0], conv_kernel.shape[1]
    fluxes = flux_read.shape[1]
    peers = crossing_bands.shape[1]
    modes, lat_count, _ = legendre_forward.shape
    cols = 2 * modes
    radius = side // 2
    assert lat_rows == 1 and lat_count == devices and devices == 2 * axes[1]
    assert layers == 2 and ocean_channels == LANES and extent % MARGIN == 0
    table = wave_table(lon, modes * devices)
    order = mode_order(lat_count, modes)
    operands = [
        atmosphere[0],
        ocean_state,
        land_mask,
        crossing_bands,
        ocean_regrid.reshape(peers, rows),
        atmosphere_regrid.reshape(peers, rows),
        surface_read[None, :],
        surface_embed[None, :],
        flux_read.T,
        flux_embed,
        legendre_forward,
        legendre_inverse,
        spectral_mix,
        conv_kernel.astype(F32).reshape(layers, side * side, ocean_channels),
        norm_gain,
        expand_weight,
        project_weight,
        atmosphere_cotangent[0],
        ocean_cotangent,
        jnp.asarray(table),
        jnp.asarray(np.ascontiguousarray(table.T)),
        jnp.asarray(order),
        jnp.asarray(np.ascontiguousarray(order.T)),
    ]
    scalars = (3, 4, 5)
    near = SLOTS // 2 * axes[0]
    shape = (rows, extent, ocean_channels)
    outs = (
        jax.ShapeDtypeStruct((lon, channels), BF16),
        jax.ShapeDtypeStruct(shape, BF16),
        jax.ShapeDtypeStruct((lon, channels), F32),
        jax.ShapeDtypeStruct(shape, F32),
    )
    window = (rows + 2 * radius, extent + 2 * MARGIN, ocean_channels)
    block = cols * devices
    vmem = pltpu.VMEM
    results = pl.pallas_call(
        functools.partial(window_kernel, axes),
        out_shape=outs,
        in_specs=[
            pl.BlockSpec(memory_space=pltpu.SMEM if index in scalars else pltpu.VMEM)
            for index in range(len(operands))
        ],
        out_specs=tuple(pl.BlockSpec(memory_space=pltpu.VMEM) for _ in outs),
        scratch_shapes=[
            vmem((2 * layers,) + window, BF16),
            vmem(window, F32),
            vmem((layers,) + shape, F32),
            vmem((layers, side * side, 8, ocean_channels), F32),
            vmem(shape, BF16),
            vmem((extent, lon), BF16),
            vmem((rows, extent), F32),
            vmem((rows, lon, ocean_channels), BF16),
            vmem((rows, fluxes, extent), F32),
            pltpu.SMEM((SLOTS, rows), F32),
            pltpu.SMEM((SLOTS, rows), F32),
            vmem((fluxes, lon), F32),
            vmem((SLOTS, fluxes, lon), F32),
            vmem((SLOTS, 1, lon), F32),
            vmem((near, 1, lon), F32),
            vmem((1, lon), F32),
            vmem((SLOTS, 1, lon), F32),
            vmem((SLOTS, fluxes, lon), F32),
            vmem((near, fluxes, lon), F32),
            vmem((4, devices, cols, channels), BF16),
            vmem((4, devices, cols, channels), BF16),
            vmem((block, channels), F32),
            vmem((lon, channels), BF16),
            vmem((block, channels), BF16),
            vmem((block, channels), BF16),
            pltpu.SemaphoreType.DMA((2 * layers, 8)),
            pltpu.SemaphoreType.DMA((2 * layers, 8)),
            pltpu.SemaphoreType.DMA((4,)),
            pltpu.SemaphoreType.DMA((4,)),
            pltpu.SemaphoreType.DMA((4, SLOTS)),
            pltpu.SemaphoreType.DMA((4,)),
        ],
        compiler_params=pltpu.CompilerParams(
            collective_id=0, has_side_effects=True, vmem_limit_bytes=60 * 1024 * 1024
        ),
    )(*operands)
    atm_next, ocean_next, atm_grad, ocean_grad = results
    return (atm_next[None], ocean_next, atm_grad[None], ocean_grad)


def solution(mesh):
    return jax.shard_map(
        per_device,
        mesh=mesh,
        in_specs=(
            P(("sec", "tile"), None, None),
            P("tile", "sec", None),
            P("tile", "sec"),
            P("tile", None),
            P("tile", None, None, None),
            P("tile", None, None, None),
            P(),
            P(),
            P(),
            P(),
            P(("sec", "tile"), None, None),
            P(("sec", "tile"), None, None),
            P(),
            P(),
            P(),
            P(),
            P(),
            P(("sec", "tile"), None, None),
            P("tile", "sec", None),
        ),
        out_specs=(
            P(("sec", "tile"), None, None),
            P("tile", "sec", None),
            P(("sec", "tile"), None, None),
            P("tile", "sec", None),
        ),
        check_vma=False,
    )
```

time: 316 us -> 152 us (0.48)
  starting transfers between devices: 67.7 us -> 0 us
  local copies, waits for them, and re-layouts: 55.2 us -> 8.76 us
  other arithmetic: 31.4 us -> 0.76 us
  Pallas kernels: 116 us -> 140 us
  matrix products: 19.9 us -> 0 us
  waiting for transfers between devices: 12.4 us -> 0 us
  blocking collectives: 10.7 us -> 0 us
    all_to_all x6 -> x0, starting transfers between devices: 43.7 us -> none  [the longest x2 18.4 us: to_bands(): lax.all_to_all(values, ('sec', 'tile'), split_axis=0, concat_axis=1, tile...]
    ppermute x16 -> x0, starting transfers between devices: 24 us -> none  [the longest x8 15.4 us: with_halo(): before = lax.ppermute(last, axis, up)]
    pallas_call x5 -> x1, Pallas kernels: 116 us -> 140 us  [per_device(): pl.pallas_call(functools.partial(window_kernel, axes), out_shape=outs, in...]
    dot_general x28 -> x0, matrix products: 19.9 us -> none  [the longest x1 2.24 us: per_device(): jnp.einsum('gk,akc->agc', table, returned, preferred_element_type=jnp.flo...]
    slice x12 -> x0, local copies, waits for them, and re-layouts: 12.1 us -> none  [the longest x2 4.2 us: with_halo(): first = lax.slice_in_dim(x, 0, width, axis=dim)]
    unnamed x88 -> x8, local copies, waits for them, and re-layouts: 18.7 us -> 6.89 us
    concatenate x5 -> x0, other arithmetic: 11.5 us -> none  [the longest x4 11.4 us: with_halo(): x = jnp.concatenate([before, x, after], axis=dim)]
    all_to_all x6 -> x0, waiting for transfers between devices: 10.7 us -> none  [the longest x2 10 us: swap(): lax.all_to_all(values, ('sec', 'tile'), split_axis=0, concat_axis=0, tile...]
  transfers between devices with their start and end apart: 22 -> 0, of which waited for: 5 -> 0; matrix products, arithmetic and copies ran while one was open for 25% -> 0% of each run, Pallas kernels for 31% -> 0%
where the time goes in v1:
time: 152 us; the launch traced here: 150 us
  Pallas kernels  140 us (92%)
  local copies, waits for them, and re-layouts  8.76 us (6%)
    pallas_call x1, Pallas kernels, per_device(): pl.pallas_call(functools.partial(window_kernel, axes), out_shape=outs, in...  140 us
    unnamed x8, local copies, waits for them, and re-layouts  6.89 us

profile of v1, /device:TPU:0, one launch (start us, length us, event | category | flops | bytes accessed | tf_op | source)
XLA Modules:
  0.0 149.7 jit_solution(17797889468425796669)
XLA Ops:
  0.6 1.2 broadcast_in_dim.13.embed
  1.9 0.8 bitcast_convert_fusion
  2.6 0.6 copy.28.taps_in
  3.3 139.5 %shard_map.246 = (bf16[360,384]{1,0:T(8,128)(2,1)}, bf16[8,720,128]{2,1,0:T(8,128)(2,1)}, f32[360,384]{1,0:T(8,128)}, f32[8,720,128]{2,1,0:T(8,128)}) custom-call(bf16[360,384]{1,0:T(8,128)(2,1)} %bitcast.12, bf16[8,720,128]{2,1,0:T(8,128)(2,1)} %ocean.1, s32[8,720]{1,0:T(8,128)} %mask.1, s32[1,4]{1,0:T(1,128)} %bands.1, f32[4,8]{1,0:T(4,128)} %bitcast.16, ...), custom_call_target="tpu_custom_call" | custom-call | tf_op jit(solution)/shard_map/pallas_call | solution.py:666
  142.8 0.0 copy-start.1
  142.8 1.7 %copy.33 = bf16[1,360,384]{2,1,0:T(8,128)(2,1)} copy(bf16[1,360,384]{2,1,0:T(8,128)(2,1)} %bitcast.14) | data formatting | bytes 552960
  144.6 0.0 copy-start
  144.6 2.7 %copy.34 = bf16[8,720,128]{2,1,0:T(8,128)(2,1)} copy(bf16[8,720,128]{2,1,0:T(8,128)(2,1)} %get-tuple-element.17) | data formatting | bytes 2949120
  147.3 0.0 copy-done.1
  147.3 0.8 copy.35
  148.1 0.0 copy-done
  148.1 1.6 %copy.36 = f32[8,720,128]{2,1,0:T(8,128)} copy(f32[8,720,128]{2,1,0:T(8,128)S(1)} %copy-done) | data formatting | bytes 5898240
Async XLA Ops:
  142.8 4.5 %copy-start.1 = (f32[360,384]{1,0:T(8,128)S(1)}, f32[360,384]{1,0:T(8,128)}, u32[]{:S(2)}) copy-start(f32[360,384]{1,0:T(8,128)} %get-tuple-element.10) | copy-start | bytes 1658884
  144.6 3.5 %copy-start = (f32[8,720,128]{2,1,0:T(8,128)S(1)}, f32[8,720,128]{2,1,0:T(8,128)}, u32[]{:S(2)}) copy-start(f32[8,720,128]{2,1,0:T(8,128)} %get-tuple-element.19) | copy-start | bytes 8847364

commit v2 on v1

--- a/solution.py
+++ b/solution.py
@@ -17,6 +17,7 @@
 MARGIN = 16
 SLOTS = 8
 LANES = 128
+STEP = 16
 
 
 def wave_table(lon_count, mode_count):
@@ -91,7 +92,7 @@
     win, wide, hid, taps, mask_wide, repeat, surf, gall, fold,
     wo, wa, flux_send, flux_recv, cp_send, cp_recv, sa_send, sa_recv, fa_send, fa_recv,
     xs, xr, flat, mixed, spec_a, spec_b,
-    halo_send, halo_recv, x_send, x_recv, near_send, near_recv,
+    halo_send, halo_recv, line_send, line_recv, x_send, x_recv, near_send, near_recv,
 ):
     sections, tiles = axes
     devices = sections * tiles
@@ -273,14 +274,45 @@
             device_id_type=MESH,
         )
 
-    def rims(layer, act, sending, row_steps):
+    def line_copy(layer, row_step, row, number):
+        place = row + rows if row_step < 0 else row - rows
+        return pltpu.make_async_remote_copy(
+            src_ref=win.at[layer, row + radius, pl.ds(MARGIN, extent)],
+            dst_ref=win.at[layer, place + radius, pl.ds(MARGIN, extent)],
+            send_sem=line_send.at[layer, number],
+            recv_sem=line_recv.at[layer, number],
+            device_id={"sec": sec, "tile": lax.rem(tile + row_step + tiles, tiles)},
+            device_id_type=MESH,
+        )
+
+    def line_start(layer, row):
+        @pl.when((row < radius) & (tile != 0))
+        def _():
+            line_copy(layer, -1, row, row).start()
+
+        @pl.when((row >= rows - radius) & (tile != tiles - 1))
+        def _():
+            line_copy(layer, 1, row, row - (rows - 2 * radius)).start()
+
+    def outer_first(body):
+        def one(index):
+            half = lax.div(index, 2)
+            body(jnp.where(lax.rem(index, 2) == 0, half, rows - 1 - half))
+
+        loop(rows, one)
+
+    def rims(layer, act, line_act, sending, row_steps):
         for row_step in row_steps:
             edge = {-1: 0, 0: None, 1: tiles - 1}[row_step if sending else -row_step]
 
             def each(row_step=row_step):
-                for col_step in (0, -1, 1):
-                    if (row_step, col_step) != (0, 0):
-                        act(rim(layer, row_step, col_step))
+                if row_step != 0 and line_act is not None:
+                    for step in range(radius):
+                        row = step if row_step < 0 else rows - radius + step
+                        number = row if row_step < 0 else row - (rows - 2 * radius)
+                        line_act(line_copy(layer, row_step, row, number))
+                for col_step in (-1, 1):
+                    act(rim(layer, row_step, col_step))
 
             if edge is None:
                 each()
@@ -288,13 +320,15 @@
                 pl.when(tile != edge)(each)
 
     def rims_start(layer):
-        rims(layer, lambda copy: copy.start(), True, (0, -1, 1))
+        rims(layer, lambda copy: copy.start(), None, True, (0, -1, 1))
 
     def rims_sent(layer):
-        rims(layer, lambda copy: copy.wait_send(), True, (0, -1, 1))
+        leave = lambda copy: copy.wait_send()
+        rims(layer, leave, leave, True, (0, -1, 1))
 
     def rims_wait(layer, row_steps):
-        rims(layer, lambda copy: copy.wait_recv(), False, row_steps)
+        arrive = lambda copy: copy.wait_recv()
+        rims(layer, arrive, arrive, False, row_steps)
 
     def widen(layer, first, count):
         def one(index):
@@ -304,27 +338,33 @@
 
     def depthwise(kernel, flip, lines, base, store):
         def step(index):
-            begin = pl.multiple_of(index * 8, 8)
+            begin = pl.multiple_of(index * STEP, STEP)
             totals = [None] * rows
             for col in range(side):
                 tap = [
                     taps[kernel, side * side - 1 - (u * side + col) if flip else u * side + col]
                     for u in range(side)
                 ]
+                partial = [None] * rows
                 for line in lines:
-                    piece = wide[line, pl.ds(begin + (MARGIN - radius + col), 8), :]
+                    piece = wide[line, pl.ds(begin + (MARGIN - radius + col), STEP), :]
+                    piece = piece.astype(BF16)
                     for u in range(side):
                         place = line - u
                         if 0 <= place < rows:
                             term = piece * tap[u]
-                            old = totals[place]
-                            totals[place] = term if old is None else old + term
+                            old = partial[place]
+                            partial[place] = term if old is None else old + term
+                for row in range(rows):
+                    if partial[row] is not None:
+                        value = partial[row].astype(F32)
+                        totals[row] = value if totals[row] is None else totals[row] + value
             for row in range(rows):
                 if totals[row] is not None:
                     before = base(row, begin)
                     store(row, begin, totals[row] if before is None else before + totals[row])
 
-        loop(extent // 8, step)
+        loop(extent // STEP, step)
 
     own_lines = range(radius, radius + rows)
     rim_lines = list(range(radius)) + list(range(radius + rows, rows + 2 * radius))
@@ -400,8 +440,8 @@
     def tap_tile(index):
         for kernel in range(taps.shape[0]):
             taps[kernel, index] = jnp.broadcast_to(
-                taps_in[kernel, pl.ds(index, 1), :], (8, channels)
-            )
+                taps_in[kernel, pl.ds(index, 1), :], (STEP, channels)
+            ).astype(BF16)
 
     loop(side * side, tap_tile)
 
@@ -418,8 +458,9 @@
         forcing = dot(repeat[...], gall[row])
         state = ocean[row].astype(F32) + mask_wide[row].astype(F32) * forcing
         win[0, row + radius, MARGIN:right, :] = state.astype(BF16)
-
-    loop(rows, force)
+        line_start(0, row)
+
+    outer_first(force)
     rims_start(0)
 
     near_wait(1, cp_recv)
@@ -446,16 +487,16 @@
             old = wide[row + radius, MARGIN:right, :]
             store(row, (old + mask_wide[row].astype(F32) * update).astype(BF16))
 
-        loop(rows, cells)
+        outer_first(cells)
 
     def hidden_store(layer):
         def store(row, begin, value):
-            hid[layer, row, pl.ds(begin, 8), :] = value
+            hid[layer, row, pl.ds(begin, STEP), :] = value
 
         return store
 
     def hidden_base(layer):
-        return lambda row, begin: hid[layer, row, pl.ds(begin, 8), :]
+        return lambda row, begin: hid[layer, row, pl.ds(begin, STEP), :]
 
     nothing = lambda row, begin: None
 
@@ -465,6 +506,7 @@
 
     def to_window(row, value):
         win[1, row + radius, MARGIN:right, :] = value
+        line_start(1, row)
 
     forward_cells(0, to_window)
     rims_start(1)
@@ -497,6 +539,7 @@
             - unit * jnp.mean(scaled * unit, axis=-1, keepdims=True)
         )
         win[window, row + radius, MARGIN:right, :] = adjoint.astype(BF16)
+        line_start(window, row)
         return before, wave
 
     def turn(row):
@@ -506,7 +549,7 @@
         old = wide[row + radius, MARGIN:right, :]
         ocean_next[row] = (old + mask_wide[row].astype(F32) * update).astype(BF16)
 
-    loop(rows, turn)
+    outer_first(turn)
     rims_start(2)
 
     all_wait(3)
@@ -521,18 +564,18 @@
     band_to_groups(2, sa_send, sa_recv, start)
 
     def grad_store(row, begin, value):
-        ocean_grad[row, pl.ds(begin, 8), :] = value
+        ocean_grad[row, pl.ds(begin, STEP), :] = value
 
     def grad_base(row, begin):
-        return ocean_grad[row, pl.ds(begin, 8), :]
+        return ocean_grad[row, pl.ds(begin, STEP), :]
 
     def given(row, begin):
-        return ocot[row, pl.ds(begin, 8), :].astype(F32)
+        return ocot[row, pl.ds(begin, STEP), :].astype(F32)
 
     first_part(2, 1, True, given, grad_store)
     second_part(2, 1, True, grad_base, grad_store)
 
-    loop(rows, lambda row: backward(0, row, hid[0, row], ocean_grad[row], 3) and None)
+    outer_first(lambda row: backward(0, row, hid[0, row], ocean_grad[row], 3) and None)
     rims_start(3)
 
     near_wait(2, sa_recv)
@@ -675,7 +718,7 @@
             vmem((2 * layers,) + window, BF16),
             vmem(window, F32),
             vmem((layers,) + shape, F32),
-            vmem((layers, side * side, 8, ocean_channels), F32),
+            vmem((layers, side * side, STEP, ocean_channels), BF16),
             vmem(shape, BF16),
             vmem((extent, lon), BF16),
             vmem((rows, extent), F32),
@@ -699,6 +742,8 @@
             vmem((block, channels), BF16),
             pltpu.SemaphoreType.DMA((2 * layers, 8)),
             pltpu.SemaphoreType.DMA((2 * layers, 8)),
+            pltpu.SemaphoreType.DMA((2 * layers, 2 * radius)),
+            pltpu.SemaphoreType.DMA((2 * layers, 2 * radius)),
             pltpu.SemaphoreType.DMA((4,)),
             pltpu.SemaphoreType.DMA((4,)),
             pltpu.SemaphoreType.DMA((4, SLOTS)),

time: 152 us -> 137 us (0.901); the launches traced: 150 us -> 136 us
  Pallas kernels: 140 us -> 126 us
    pallas_call x1, Pallas kernels: 140 us -> 126 us  [per_device(): pl.pallas_call(functools.partial(window_kernel, axes), out_shape=outs, in...]
where the time goes in v2:
time: 137 us; the launch traced here: 136 us
  Pallas kernels  126 us (92%)
  local copies, waits for them, and re-layouts  8.76 us (6%)
    pallas_call x1, Pallas kernels, per_device(): pl.pallas_call(functools.partial(window_kernel, axes), out_shape=outs, in...  126 us
    unnamed x8, local copies, waits for them, and re-layouts  6.89 us

profile of v2, /device:TPU:0, one launch (start us, length us, event | category | flops | bytes accessed | tf_op | source)
XLA Modules:
  0.0 136.3 jit_solution(12886179899091774598)
XLA Ops:
  0.6 1.2 broadcast_in_dim.13.embed
  1.9 0.8 bitcast_convert_fusion
  2.6 0.6 copy.28.taps_in
  3.3 126.2 %shard_map.246 = (bf16[360,384]{1,0:T(8,128)(2,1)}, bf16[8,720,128]{2,1,0:T(8,128)(2,1)}, f32[360,384]{1,0:T(8,128)}, f32[8,720,128]{2,1,0:T(8,128)}) custom-call(bf16[360,384]{1,0:T(8,128)(2,1)} %bitcast.12, bf16[8,720,128]{2,1,0:T(8,128)(2,1)} %ocean.1, s32[8,720]{1,0:T(8,128)} %mask.1, s32[1,4]{1,0:T(1,128)} %bands.1, f32[4,8]{1,0:T(4,128)} %bitcast.16, ...), custom_call_target="tpu_custom_call" | custom-call | tf_op jit(solution)/shard_map/pallas_call | solution.py:709
  129.4 0.0 copy-start.1
  129.4 1.7 %copy.33 = bf16[1,360,384]{2,1,0:T(8,128)(2,1)} copy(bf16[1,360,384]{2,1,0:T(8,128)(2,1)} %bitcast.14) | data formatting | bytes 552960
  131.2 0.0 copy-start
  131.2 2.7 %copy.34 = bf16[8,720,128]{2,1,0:T(8,128)(2,1)} copy(bf16[8,720,128]{2,1,0:T(8,128)(2,1)} %get-tuple-element.17) | data formatting | bytes 2949120
  133.9 0.0 copy-done.1
  133.9 0.8 copy.35
  134.7 0.0 copy-done
  134.7 1.6 %copy.36 = f32[8,720,128]{2,1,0:T(8,128)} copy(f32[8,720,128]{2,1,0:T(8,128)S(1)} %copy-done) | data formatting | bytes 5898240
Async XLA Ops:
  129.4 4.5 %copy-start.1 = (f32[360,384]{1,0:T(8,128)S(1)}, f32[360,384]{1,0:T(8,128)}, u32[]{:S(2)}) copy-start(f32[360,384]{1,0:T(8,128)} %get-tuple-element.10) | copy-start | bytes 1658884
  131.2 3.5 %copy-start = (f32[8,720,128]{2,1,0:T(8,128)S(1)}, f32[8,720,128]{2,1,0:T(8,128)}, u32[]{:S(2)}) copy-start(f32[8,720,128]{2,1,0:T(8,128)} %get-tuple-element.19) | copy-start | bytes 8847364

commit v3 on v2

--- a/solution.py
+++ b/solution.py
@@ -80,7 +80,7 @@
 
 def gelu_slope(before, square, wave):
     slope = (0.5 * GELU_SCALE + (1.5 * GELU_SCALE * GELU_CUBIC) * square) * before
-    return 0.5 + 0.5 * wave + slope * (1.0 - wave * wave)
+    return (1.0 + wave) * (0.5 + slope * (1.0 - wave))
 
 
 def window_kernel(
@@ -437,13 +437,11 @@
     for row in range(rows):
         mask_wide[row] = column[:, row * LANES : (row + 1) * LANES].astype(BF16)
 
-    def tap_tile(index):
-        for kernel in range(taps.shape[0]):
-            taps[kernel, index] = jnp.broadcast_to(
-                taps_in[kernel, pl.ds(index, 1), :], (STEP, channels)
-            ).astype(BF16)
-
-    loop(side * side, tap_tile)
+    for kernel in range(taps.shape[0]):
+        for u in range(side):
+            for v in range(side):
+                tile_of = jnp.broadcast_to(taps_in[kernel, u, v : v + 1, :], (STEP, channels))
+                taps[kernel, u * side + v] = tile_of.astype(BF16)
 
     near_wait(0, flux_recv)
     for row in range(rows):
@@ -480,9 +478,9 @@
         def cells(row):
             unit, _ = normalize(hid[layer, row])
             normed = (unit * gains[layer : layer + 1, :]).astype(BF16)
-            before = dot(normed, expand[layer])
+            before = dot(normed, expand[layer]).astype(BF16)
             _, wave = gelu_parts(before)
-            active = gelu_value(before, wave).astype(BF16)
+            active = gelu_value(before, wave)
             update = dot(active, project[layer])
             old = wide[row + radius, MARGIN:right, :]
             store(row, (old + mask_wide[row].astype(F32) * update).astype(BF16))
@@ -527,11 +525,11 @@
         gain = gains[layer : layer + 1, :]
         unit, inverse_std = normalize(hidden)
         normed = (unit * gain).astype(BF16)
-        before = dot(normed, expand[layer])
+        before = dot(normed, expand[layer]).astype(BF16)
         masked = (mask_wide[row].astype(F32) * cotangent).astype(BF16)
-        active_adjoint = dot_nt(masked, project[layer])
+        active_adjoint = dot_nt(masked, project[layer]).astype(BF16)
         square, wave = gelu_parts(before)
-        before_adjoint = (gelu_slope(before, square, wave) * active_adjoint).astype(BF16)
+        before_adjoint = gelu_slope(before, square, wave) * active_adjoint
         scaled = dot_nt(before_adjoint, expand[layer]) * gain
         adjoint = inverse_std * (
             scaled
@@ -544,7 +542,7 @@
 
     def turn(row):
         before, wave = backward(1, row, hid[1, row], ocot[row].astype(F32), 2)
-        active = gelu_value(before, wave).astype(BF16)
+        active = gelu_value(before, wave)
         update = dot(active, project[1])
         old = wide[row + radius, MARGIN:right, :]
         ocean_next[row] = (old + mask_wide[row].astype(F32) * update).astype(BF16)
@@ -632,6 +630,29 @@
         all_sent(index)
     for layer in range(win.shape[0]):
         rims_sent(layer)
+
+
+def hand_over(*refs):
+    count = (len(refs) - 2) // 3
+    given, results, held = refs[:count], refs[count : 2 * count], refs[2 * count : 3 * count]
+    arrived, left = refs[3 * count], refs[3 * count + 1]
+    pieces = []
+    for index in range(count):
+        parts = given[index].shape[0] if len(given[index].shape) == 3 else 1
+        for part in range(parts):
+            at = (part,) if parts > 1 else (Ellipsis,)
+            source, middle, place = (
+                ref.at[at] for ref in (given[index], held[index], results[index])
+            )
+            first = pltpu.make_async_copy(source, middle, arrived.at[index, part])
+            second = pltpu.make_async_copy(middle, place, left.at[index, part])
+            first.start()
+            pieces.append((first, second))
+    for first, second in pieces:
+        first.wait()
+        second.start()
+    for _, second in pieces:
+        second.wait()
 
 
 def per_device(
@@ -677,13 +698,13 @@
         ocean_regrid.reshape(peers, rows),
         atmosphere_regrid.reshape(peers, rows),
         surface_read[None, :],
-        surface_embed[None, :],
+        surface_embed.reshape(1, channels),
         flux_read.T,
         flux_embed,
         legendre_forward,
         legendre_inverse,
         spectral_mix,
-        conv_kernel.astype(F32).reshape(layers, side * side, ocean_channels),
+        conv_kernel,
         norm_gain,
         expand_weight,
         project_weight,
@@ -753,6 +774,14 @@
             collective_id=0, has_side_effects=True, vmem_limit_bytes=60 * 1024 * 1024
         ),
     )(*operands)
+    results = pl.pallas_call(
+        hand_over,
+        out_shape=outs,
+        in_specs=[pl.BlockSpec(memory_space=pl.ANY) for _ in outs],
+        out_specs=tuple(pl.BlockSpec(memory_space=pl.ANY) for _ in outs),
+        scratch_shapes=[vmem(out.shape, out.dtype) for out in outs]
+        + [pltpu.SemaphoreType.DMA((len(outs), rows))] * 2,
+    )(*results)
     atm_next, ocean_next, atm_grad, ocean_grad = results
     return (atm_next[None], ocean_next, atm_grad[None], ocean_grad)
 

time: 137 us -> 130 us (0.949)
  local copies, waits for them, and re-layouts: 8.76 us -> 2.6 us
    unnamed x8 -> x1, local copies, waits for them, and re-layouts: 6.89 us -> 1.35 us
    pallas_call x0 -> x1, Pallas kernels: none -> 5.2 us  [per_device(): pl.pallas_call(hand_over, out_shape=outs, in_specs=[pl.BlockSpec(memory_s...]
    pallas_call x1, Pallas kernels: 126 us -> 121 us  [per_device(): pl.pallas_call(functools.partial(window_kernel, axes), out_shape=outs, in...]
where the time goes in v3:
time: 130 us
  Pallas kernels  126 us (97%)
  local copies, waits for them, and re-layouts  2.6 us (2%)
    pallas_call x1, Pallas kernels, per_device(): pl.pallas_call(functools.partial(window_kernel, axes), out_shape=outs, in...  121 us
    pallas_call x1, Pallas kernels, per_device(): pl.pallas_call(hand_over, out_shape=outs, in_specs=[pl.BlockSpec(memory_s...  5.2 us

profile of v3, /device:TPU:0, one launch (start us, length us, event | category | flops | bytes accessed | tf_op | source)
XLA Modules:
  0.0 129.7 jit_solution(15670630325138293605)
XLA Ops:
  0.6 1.2 reshape.19.embed
  1.9 1.4 %copy.27.taps_in = bf16[2,7,7,128]{3,2,1,0:T(8,128)(2,1)} copy(bf16[2,7,7,128]{3,0,2,1:T(2,128)(2,1)} %param.36) | data formatting | bytes 50176 | tf_op args[13]
  3.2 121.3 %shard_map.246 = (bf16[360,384]{1,0:T(8,128)(2,1)}, bf16[8,720,128]{2,1,0:T(8,128)(2,1)}, f32[360,384]{1,0:T(8,128)}, f32[8,720,128]{2,1,0:T(8,128)}) custom-call(bf16[360,384]{1,0:T(8,128)(2,1)} %bitcast.8, bf16[8,720,128]{2,1,0:T(8,128)(2,1)} %ocean.1, s32[8,720]{1,0:T(8,128)} %mask.1, s32[1,4]{1,0:T(1,128)} %bands.1, f32[4,8]{1,0:T(4,128)} %bitcast.11, ...), custom_call_target="tpu_custom_call" | custom-call | tf_op jit(solution)/shard_map/pallas_call | solution.py:730
  124.5 5.2 %shard_map.247 = (bf16[360,384]{1,0:T(8,128)(2,1)}, bf16[8,720,128]{2,1,0:T(8,128)(2,1)}, f32[360,384]{1,0:T(8,128)}, f32[8,720,128]{2,1,0:T(8,128)}) custom-call(bf16[360,384]{1,0:T(8,128)(2,1)} %get-tuple-element.12.refs_0_, bf16[8,720,128]{2,1,0:T(8,128)(2,1)} %get-tuple-element.13.refs_1_, f32[360,384]{1,0:T(8,128)} %get-tuple-element.14.refs_2_, ...), custom_call_target="tpu_custom_call" | custom-call | tf_op jit(solution)/shard_map/pallas_call | solution.py:777

commit v4 on v3

--- a/solution.py
+++ b/solution.py
@@ -83,8 +83,23 @@
     return (1.0 + wave) * (0.5 + slope * (1.0 - wave))
 
 
+def staged_kernel(axes, late, total, *refs):
+    ins, held, arrived = list(refs[:total]), refs[-1 - len(late) : -1], refs[-1]
+    copies = []
+    for place, index in enumerate(late):
+        copies.append(pltpu.make_async_copy(ins[index], held[place], arrived.at[place]))
+        copies[-1].start()
+        ins[index] = held[place]
+
+    def ready():
+        for copy in copies:
+            copy.wait()
+
+    window_kernel(axes, ready, *ins, *refs[total : -1 - len(late)])
+
+
 def window_kernel(
-    axes,
+    axes, ready,
     atm, ocean, mask, bands, oreg, areg, read, embed, flux_read_t, flux_embed,
     leg_f, leg_i, smix, taps_in, gains, expand, project, acot, ocot,
     table, table_t, order, order_t,
@@ -164,6 +179,7 @@
     loop(SLOTS, coarse_part)
 
     pl.semaphore_wait(barrier, devices - 1)
+    ready()
 
     def band_to_groups(index, source, slots, act):
         def one(step):
@@ -345,7 +361,8 @@
                     taps[kernel, side * side - 1 - (u * side + col) if flip else u * side + col]
                     for u in range(side)
                 ]
-                partial = [None] * rows
+                if col % 2 == 0:
+                    partial = [None] * rows
                 for line in lines:
                     piece = wide[line, pl.ds(begin + (MARGIN - radius + col), STEP), :]
                     piece = piece.astype(BF16)
@@ -356,7 +373,7 @@
                             old = partial[place]
                             partial[place] = term if old is None else old + term
                 for row in range(rows):
-                    if partial[row] is not None:
+                    if partial[row] is not None and (col % 2 == 1 or col == side - 1):
                         value = partial[row].astype(F32)
                         totals[row] = value if totals[row] is None else totals[row] + value
             for row in range(rows):
@@ -716,6 +733,7 @@
         jnp.asarray(np.ascontiguousarray(order.T)),
     ]
     scalars = (3, 4, 5)
+    late = (10, 11, 12, 15, 16, 17, 18, 19, 20, 21, 22)
     near = SLOTS // 2 * axes[0]
     shape = (rows, extent, ocean_channels)
     outs = (
@@ -728,10 +746,14 @@
     block = cols * devices
     vmem = pltpu.VMEM
     results = pl.pallas_call(
-        functools.partial(window_kernel, axes),
+        functools.partial(staged_kernel, axes, late, len(operands)),
         out_shape=outs,
         in_specs=[
-            pl.BlockSpec(memory_space=pltpu.SMEM if index in scalars else pltpu.VMEM)
+            pl.BlockSpec(
+                memory_space=pltpu.SMEM
+                if index in scalars
+                else pl.ANY if index in late else pltpu.VMEM
+            )
             for index in range(len(operands))
         ],
         out_specs=tuple(pl.BlockSpec(memory_space=pltpu.VMEM) for _ in outs),
@@ -769,7 +791,9 @@
             pltpu.SemaphoreType.DMA((4,)),
             pltpu.SemaphoreType.DMA((4, SLOTS)),
             pltpu.SemaphoreType.DMA((4,)),
-        ],
+        ]
+        + [vmem(operands[index].shape, operands[index].dtype) for index in late]
+        + [pltpu.SemaphoreType.DMA((len(late),))],
         compiler_params=pltpu.CompilerParams(
             collective_id=0, has_side_effects=True, vmem_limit_bytes=60 * 1024 * 1024
         ),

time: 130 us -> 127 us (0.977)
  Pallas kernels: 126 us -> 123 us
    pallas_call x1, Pallas kernels: 121 us -> 118 us  [per_device(): pl.pallas_call(functools.partial(staged_kernel, axes, late, len(operands)...]
where the time goes in v4:
time: 127 us
  Pallas kernels  123 us (97%)
  local copies, waits for them, and re-layouts  2.6 us (2%)
    pallas_call x1, Pallas kernels, per_device(): pl.pallas_call(functools.partial(staged_kernel, axes, late, len(operands)...  118 us
    pallas_call x1, Pallas kernels, per_device(): pl.pallas_call(hand_over, out_shape=outs, in_specs=[pl.BlockSpec(memory_s...  5.2 us

profile of v4, /device:TPU:0, one launch (start us, length us, event | category | flops | bytes accessed | tf_op | source)
XLA Modules:
  0.0 126.5 jit_solution(10407264646696926081)
XLA Ops:
  0.6 1.2 reshape.19.refs_7_
  1.9 1.4 %copy.27.refs_13_ = bf16[2,7,7,128]{3,2,1,0:T(8,128)(2,1)} copy(bf16[2,7,7,128]{3,0,2,1:T(2,128)(2,1)} %param.36) | data formatting | bytes 50176 | tf_op args[13]
  3.2 118.1 %shard_map.246 = (bf16[360,384]{1,0:T(8,128)(2,1)}, bf16[8,720,128]{2,1,0:T(8,128)(2,1)}, f32[360,384]{1,0:T(8,128)}, f32[8,720,128]{2,1,0:T(8,128)}) custom-call(bf16[360,384]{1,0:T(8,128)(2,1)} %bitcast.8, bf16[8,720,128]{2,1,0:T(8,128)(2,1)} %refs_1_.1, s32[8,720]{1,0:T(8,128)} %refs_2_.1, s32[1,4]{1,0:T(1,128)} %refs_3_.1, f32[4,8]{1,0:T(4,128)} %bitcast.11, ...), custom_call_target="tpu_custom_call" | custom-call | tf_op jit(solution)/shard_map/pallas_call | solution.py:748
  121.3 5.2 %shard_map.247 = (bf16[360,384]{1,0:T(8,128)(2,1)}, bf16[8,720,128]{2,1,0:T(8,128)(2,1)}, f32[360,384]{1,0:T(8,128)}, f32[8,720,128]{2,1,0:T(8,128)}) custom-call(bf16[360,384]{1,0:T(8,128)(2,1)} %get-tuple-element.12.refs_0_, bf16[8,720,128]{2,1,0:T(8,128)(2,1)} %get-tuple-element.13.refs_1_, f32[360,384]{1,0:T(8,128)} %get-tuple-element.14.refs_2_, ...), custom_call_target="tpu_custom_call" | custom-call | tf_op jit(solution)/shard_map/pallas_call | solution.py:801
